TPU v7x, 16 devices: a 4x2x1 block of a 4x4x8 slice. The times are simulated.
16 devices in a mesh: dp: 2 (over y, z), tp: 8 (over x, core).
Axes of the slice: x: 4, y: 2, z: 1, core: 2. Of those that a mesh axis runs over, the one named last changes fastest.
The devices are a block of a 4x4x8 slice.
Arguments:
- x: bfloat16 [24, 256, 5120], P('dp', 'tp'), parts along dimension 0
- k_cache: bfloat16 [24, 1024, 8, 128], P('dp', None, 'tp'), parts along dimension 0
- v_cache: bfloat16 [24, 1024, 8, 128], P('dp', None, 'tp'), parts along dimension 0
- prefix_len: int32 [24], P('dp'), parts along dimension 0
- valid_len: int32 [24], P('dp'), parts along dimension 0
- g_attn: bfloat16 [5120], replicated
- w_q: bfloat16 [5120, 5120], P(None, 'tp')
- b_q: bfloat16 [5120], P('tp')
- w_k: bfloat16 [5120, 1024], P(None, 'tp')
- b_k: bfloat16 [1024], P('tp')
- w_v: bfloat16 [5120, 1024], P(None, 'tp')
- b_v: bfloat16 [1024], P('tp')
- w_o: bfloat16 [5120, 5120], P('tp')
- g_mlp: bfloat16 [5120], replicated
- w_gate: bfloat16 [5120, 27648], P(None, 'tp')
- w_up: bfloat16 [5120, 27648], P(None, 'tp')
- w_down: bfloat16 [27648, 5120], P('tp')
Outputs:
- output 1: bfloat16 [24, 256, 5120], P('dp', 'tp'), parts along dimension 0
- output 2: bfloat16 [24, 1024, 8, 128], P('dp', None, 'tp'), parts along dimension 0
- output 3: bfloat16 [24, 1024, 8, 128], P('dp', None, 'tp'), parts along dimension 0
There are 2 independent parts. A program takes and returns all parts, laid end to end along the dimension named above; an argument that names none is the same for every part.
All inputs are finite; a program needn't handle non-finite values.
Results may differ from a plain program's by a relative error of at most 0.0193666.
Values are sent between devices in bfloat16 or wider.
A program may use at most 768 MiB of HBM per device.

v0:
```python
import jax
import jax.numpy as jnp
from jax import lax
from jax.sharding import PartitionSpec as P

ROPE_THETA = 1.0e6
NORM_EPS = 1.0e-6


def rms_norm(hidden, gain):
    wide_vals = hidden.astype(jnp.float32)
    inv_rms = lax.rsqrt(jnp.mean(wide_vals * wide_vals, axis=-1, keepdims=True) + NORM_EPS)
    return (wide_vals * inv_rms * gain.astype(jnp.float32)).astype(jnp.bfloat16)


def rotate_heads(heads, positions):
    half = heads.shape[-1] // 2
    inv_freq = ROPE_THETA ** (-(jnp.arange(half, dtype=jnp.float32) * 2.0) / heads.shape[-1])
    angles = positions.astype(jnp.float32)[..., None] * inv_freq
    cos_t = jnp.cos(angles)[..., None, :]
    sin_t = jnp.sin(angles)[..., None, :]
    wide = heads.astype(jnp.float32)
    first_half = wide[..., :half]
    second_half = wide[..., half:]
    rotated = jnp.concatenate([first_half * cos_t - second_half * sin_t, second_half * cos_t + first_half * sin_t], axis=-1)
    return rotated.astype(jnp.bfloat16)


def project(hidden, weight, bias):
    total = jnp.einsum("rcd,dn->rcn", hidden, weight, preferred_element_type=jnp.float32)
    return (total + bias.astype(jnp.float32)).astype(jnp.bfloat16)


def write_rows(cache, new_rows, prefix, valid):
    n_tokens = new_rows.shape[1]
    row_ids = jnp.arange(n_tokens, dtype=jnp.int32)[None, :, None, None]
    window = (1, n_tokens, cache.shape[2], cache.shape[3])

    def body(req_idx, buffer):
        start = prefix[req_idx]
        old_rows = lax.dynamic_slice(buffer, (req_idx, start, 0, 0), window)
        fresh = lax.dynamic_slice_in_dim(new_rows, req_idx, 1, axis=0)
        merged = jnp.where(row_ids < valid[req_idx], fresh, old_rows)
        return lax.dynamic_update_slice(buffer, merged, (req_idx, start, 0, 0))

    return lax.fori_loop(0, cache.shape[0], body, cache)


def attend(queries, k_cache, v_cache, prefix, valid):
    n_req, n_tokens, q_heads, head_dim = queries.shape
    slots, kv_local = k_cache.shape[1], k_cache.shape[2]
    query_groups = queries.reshape(n_req, n_tokens, kv_local, q_heads // kv_local, head_dim)
    scores = jnp.einsum("rckgd,rskd->rkgcs", query_groups, k_cache, preferred_element_type=jnp.float32) * (head_dim ** -0.5)
    row_ids = jnp.arange(n_tokens, dtype=jnp.int32)
    limit = prefix[:, None] + jnp.minimum(row_ids[None, :], valid[:, None] - 1)
    visible = jnp.arange(slots, dtype=jnp.int32)[None, None, :] <= limit[:, :, None]
    scores = jnp.where(visible[:, None, None], scores, -1.0e30)
    attn_probs = jax.nn.softmax(scores, axis=-1).astype(jnp.bfloat16)
    mixed = jnp.einsum("rkgcs,rskd->rckgd", attn_probs, v_cache, preferred_element_type=jnp.float32)
    return mixed.astype(jnp.bfloat16).reshape(n_req, n_tokens, q_heads * head_dim)


def attention_heads(normed_full, k_cache, v_cache, prefix, valid, w_q, b_q, w_k, b_k, w_v, b_v):
    n_req, n_tokens = normed_full.shape[0], normed_full.shape[1]
    head_dim = k_cache.shape[-1]
    positions = prefix[:, None] + jnp.arange(n_tokens, dtype=jnp.int32)[None, :]
    queries = rotate_heads(project(normed_full, w_q, b_q).reshape(n_req, n_tokens, -1, head_dim), positions)
    keys_new = rotate_heads(project(normed_full, w_k, b_k).reshape(n_req, n_tokens, -1, head_dim), positions)
    values_new = project(normed_full, w_v, b_v).reshape(n_req, n_tokens, -1, head_dim)
    k_out = write_rows(k_cache, keys_new, prefix, valid)
    v_out = write_rows(v_cache, values_new, prefix, valid)
    return attend(queries, k_out, v_out, prefix, valid), k_out, v_out


def mlp_partial(normed_full, w_gate, w_up, w_down):
    gate = jnp.einsum("rcd,df->rcf", normed_full, w_gate, preferred_element_type=jnp.float32)
    up_proj = jnp.einsum("rcd,df->rcf", normed_full, w_up, preferred_element_type=jnp.float32)
    hidden_act = (jax.nn.silu(gate) * up_proj).astype(jnp.bfloat16)
    return jnp.einsum("rcf,fd->rcd", hidden_act, w_down, preferred_element_type=jnp.float32).astype(jnp.bfloat16)


def add_rounded(first, second):
    return (first.astype(jnp.float32) + second.astype(jnp.float32)).astype(jnp.bfloat16)


def solution(mesh):
    row_spec = P("dp", "tp", None)
    cache_spec = P("dp", None, "tp", None)
    req_spec = P("dp")
    rep_spec = P(None)
    col_spec = P(None, "tp")
    bias_spec = P("tp")
    down_spec = P("tp", None)

    def layer(x_rows, k_cache, v_cache, prefix, valid, g_attn, w_q, b_q, w_k, b_k, w_v, b_v, w_o, g_mlp, w_gate, w_up, w_down):
        normed = rms_norm(x_rows, g_attn)
        normed_full = lax.all_gather(normed, "tp", axis=1, tiled=True)
        attended, k_out, v_out = attention_heads(normed_full, k_cache, v_cache, prefix, valid, w_q, b_q, w_k, b_k, w_v, b_v)
        attn_part = jnp.einsum("rcn,nd->rcd", attended, w_o, preferred_element_type=jnp.float32).astype(jnp.bfloat16)
        attn_rows = lax.psum_scatter(attn_part, "tp", scatter_dimension=1, tiled=True)
        resid_mid = add_rounded(x_rows, attn_rows)
        normed_mlp = rms_norm(resid_mid, g_mlp)
        mlp_full = lax.all_gather(normed_mlp, "tp", axis=1, tiled=True)
        down_part = mlp_partial(mlp_full, w_gate, w_up, w_down)
        down_rows = lax.psum_scatter(down_part, "tp", scatter_dimension=1, tiled=True)
        return add_rounded(resid_mid, down_rows), k_out, v_out

    in_specs = (row_spec, cache_spec, cache_spec, req_spec, req_spec, rep_spec, col_spec, bias_spec, col_spec, bias_spec, col_spec, bias_spec, down_spec, rep_spec, col_spec, col_spec, down_spec)
    return jax.shard_map(layer, mesh=mesh, in_specs=in_specs, out_specs=(row_spec, cache_spec, cache_spec), check_vma=False)
```

profile of v0, /device:TPU:112, one launch (start us, length us, event | category | flops | bytes accessed | tf_op | source)
XLA Modules:
  0.0 1425.2 jit_solution(12025085518315355211)
XLA Ops:
  19.6 6.8 multiply_cosine_fusion
  30.0 135.8 %all-gather.3.cloned.1.call-done = bf16[12,256,5120]{2,1,0:T(8,128)(2,1)} async-done(((bf16[12,32,5120]{2,1,0:T(8,128)(2,1)}), bf16[12,256,5120]{2,1,0:T(8,128)(2,1)}) %all-gather.3.cloned.1.call-update) | async-done | bytes 31457296 | tf_op jit(solution)/shard_map/all_gather | solution.py:97
  165.8 15.2 %fusion.46 = bf16[12,256,1,128]{3,1,2,0:T(8,128)(2,1)} fusion(bf16[12,256,5120]{2,1,0:T(8,128)(2,1)} %all-gather.3.cloned.1.call-done, bf16[5120,128]{1,0:T(8,128)(2,1)S(1)} %copy-done, f32[128]{0:T(128)S(1)} %convert_element_type.106), kind=kOutput, calls=%fused_computation.58 | convolution fusion | flops 4027318272 | bytes 33554944 | tf_op jit(solution)/shard_map/rcd,dn->rcn/dot_general | solution.py:30
  181.0 80.2 %while.28 = (s32[]{:T(128)}, bf16[12,1024,1,128]{3,1,2,0:T(8,128)(2,1)}, s32[12]{0:T(128)S(1)}, bf16[12,256,1,128]{3,1,2,0:T(8,128)(2,1)}, s32[12]{0:T(128)S(1)}, /*index=5*/s32[]{:T(128)}, s32[]{:T(128)}, s32[]{:T(128)}) while((s32[]{:T(128)}, bf16[12,1024,1,128]{3,1,2,0:T(8,128)(2,1)}, s32[12]{0:T(128)S(1)}, ...), condition=%wide.region_2.3_spmd.clone, body=%wide.region_1.2_spmd.clone.sunk | while | flops 33029 | bytes 328359 | solution.py:46
  261.2 15.5 %fusion.52 = f32[12,256,1,128]{1,3,0,2:T(8,128)S(1)} fusion(bf16[12,256,5120]{2,1,0:T(8,128)(2,1)} %all-gather.3.cloned.1.call-done, bf16[5120,128]{1,0:T(8,128)(2,1)} %param.29, f32[128]{0:T(128)S(1)} %convert_element_type.108), kind=kOutput, calls=%fused_computation.60 | convolution fusion | flops 4027711488 | bytes 34341376 | tf_op jit(solution)/shard_map/rcd,dn->rcn/dot_general | solution.py:30
  280.0 31.7 %fusion.30 = f32[12,256,640]{2,1,0:T(8,128)} fusion(f32[640]{0:T(1024)S(1)} %convert_element_type.113, bf16[12,256,5120]{2,1,0:T(8,128)(2,1)} %all-gather.3.cloned.1.call-done, bf16[5120,640]{1,0:T(8,128)(2,1)} %param.27), kind=kOutput, calls=%fused_computation.44 | convolution fusion | flops 20138557440 | bytes 45877760 | tf_op jit(solution)/shard_map/rcd,dn->rcn/dot_general | solution.py:30
  311.7 9.1 copy.31
  320.8 7.6 fusion.66
  328.4 79.1 %while.29 = (s32[]{:T(128)}, bf16[12,1024,1,128]{3,1,2,0:T(8,128)(2,1)}, s32[12]{0:T(128)S(1)}, bf16[12,256,1,128]{1,3,0,2:T(8,128)(2,1)S(1)}, s32[12]{0:T(128)S(1)}, /*index=5*/s32[]{:T(128)}, s32[]{:T(128)}, s32[]{:T(128)}) while((s32[]{:T(128)}, bf16[12,1024,1,128]{3,1,2,0:T(8,128)(2,1)}, s32[12]{0:T(128)S(1)}, ...), condition=%wide.region_4.5_spmd.clone, body=%wide.region_3.4_spmd.clone.sunk | while | flops 33029 | bytes 590507 | solution.py:46
  407.5 6.6 copy.47
  414.1 6.6 copy.46
  420.7 9.8 subtract_convert_fusion
  430.5 28.5 %fusion.5 = (f32[12,5,256]{2,1,0:T(8,128)S(1)}, f32[12,1024,256,5]{2,1,3,0:T(8,128)}) fusion(pred[12,256,1024]{1,2,0:T(8,128)(4,1)} %iota_compare_fusion, bf16[12,256,5,64]{3,1,2,0:T(8,128)(2,1)} %get-tuple-element.288, bf16[12,256,5,64]{3,1,2,0:T(8,128)(2,1)} %get-tuple-element.287, bf16[12,1024,1,128]{3,1,2,0:T(8,128)(2,1)} %get-tuple-element.219), kind=kOutput, calls=%fused_computation.11 | convolution fusion | flops 4081566720 | bytes 73199616 | tf_op jit(solution)/shard_map/rckgd,rskd->rkgcs/dot_general | solution.py:53
  458.9 21.2 %fusion.4 = f32[12,5,256]{2,1,0:T(8,128)S(1)} fusion(f32[12,1024,256,5]{2,1,3,0:T(8,128)} %get-tuple-element.298, f32[12,5,256]{2,1,0:T(8,128)S(1)} %get-tuple-element.297, pred[12,256,1024]{1,2,0:T(8,128)(4,1)} %iota_compare_fusion), kind=kLoop, calls=%fused_computation.10 | loop fusion | flops 62899200 | bytes 66183168 | tf_op jit(solution)/shard_map/reduce_sum | solution.py:58
  480.2 27.9 %fusion.39 = bf16[12,128,5,256]{3,1,2,0:T(8,128)(2,1)} fusion(f32[12,5,256]{2,1,0:T(8,128)S(1)} %fusion.4, f32[12,5,256]{2,1,0:T(8,128)S(1)} %get-tuple-element.297, f32[12,1024,256,5]{2,1,3,0:T(8,128)} %get-tuple-element.298, pred[12,256,1024]{1,2,0:T(8,128)(4,1)} %iota_compare_fusion, bf16[12,1024,1,128]{3,1,2,0:T(8,128)(2,1)} %get-tuple-element.220), kind=kOutput, calls=%fused_computation.51 | convolution fusion | flops 4107141120 | bytes 73261056 | tf_op jit(solution)/shard_map/rkgcs,rskd->rckgd/dot_general | solution.py:59
  508.0 32.6 %convolution_convert_fusion = bf16[12,256,5120]{2,1,0:T(8,128)(2,1)} fusion(bf16[12,256,640]{1,2,0:T(8,128)(2,1)} %bitcast.105, bf16[640,5120]{1,0:T(8,128)(2,1)} %param.33), kind=kOutput, calls=%fused_computation.21 | convolution fusion | flops 20148387840 | bytes 41943040 | tf_op jit(solution)/shard_map/rcn,nd->rcd/dot_general | solution.py:99
  541.3 157.6 %reduce-scatter.3.cloned.1.call-done = bf16[12,32,5120]{2,1,0:T(8,128)(2,1)} async-done(((bf16[12,256,5120]{2,1,0:T(8,128)(2,1)}), bf16[12,32,5120]{2,1,0:T(8,128)(2,1)}) %reduce-scatter.3.cloned.1.call-update) | async-done | bytes 3932176 | tf_op jit(solution)/shard_map/reduce_scatter | solution.py:100
  699.0 4.8 fusion.23
  708.6 143.4 %all-gather.5.cloned.1.call-done = bf16[12,256,5120]{2,1,0:T(8,128)(2,1)} async-done(((bf16[12,32,5120]{2,1,0:T(8,128)(2,1)}), bf16[12,256,5120]{2,1,0:T(8,128)(2,1)}) %all-gather.5.cloned.1.call-update) | async-done | bytes 31457296 | tf_op jit(solution)/shard_map/all_gather | solution.py:103
  852.0 125.6 %fusion.8 = f32[12,256,3456]{2,1,0:T(8,128)} fusion(bf16[12,256,5120]{2,1,0:T(8,128)(2,1)} %all-gather.5.cloned.1.call-done, bf16[5120,3456]{1,0:T(8,128)(2,1)} %param.36), kind=kOutput, calls=%fused_computation.15 | convolution fusion | flops 108716359680 | bytes 109314048 | tf_op jit(solution)/shard_map/rcd,df->rcf/dot_general | solution.py:77
  977.6 149.6 %multiply_convert_fusion = bf16[12,256,3456]{2,1,0:T(8,128)(2,1)} fusion(f32[12,256,3456]{2,1,0:T(8,128)} %fusion.8, bf16[12,256,5120]{2,1,0:T(8,128)(2,1)} %all-gather.5.cloned.1.call-done, bf16[5120,3456]{1,0:T(8,128)(2,1)} %param.35), kind=kOutput, calls=%fused_computation.12 | convolution fusion | flops 108780060672 | bytes 130547712 | tf_op jit(solution)/shard_map/rcd,df->rcf/dot_general | solution.py:76
  1127.2 124.5 %fusion.16 = bf16[12,256,5120]{2,1,0:T(8,128)(2,1)} fusion(bf16[12,256,3456]{2,1,0:T(8,128)(2,1)} %multiply_convert_fusion, bf16[3456,5120]{1,0:T(8,128)(2,1)} %param.37), kind=kOutput, calls=%fused_computation.22 | convolution fusion | flops 108732088320 | bytes 88080384 | tf_op jit(solution)/shard_map/rcf,fd->rcd/dot_general | solution.py:79
  1251.8 158.1 %reduce-scatter.5.cloned.1.call-done = bf16[12,32,5120]{2,1,0:T(8,128)(2,1)} async-done(((bf16[12,256,5120]{2,1,0:T(8,128)(2,1)}), bf16[12,32,5120]{2,1,0:T(8,128)(2,1)}) %reduce-scatter.5.cloned.1.call-update) | async-done | bytes 3932176 | tf_op jit(solution)/shard_map/reduce_scatter | solution.py:105
  1409.8 8.5 fusion.26
  (194 shorter events, 136.0 us)
Async XLA Ops:
  7.2 158.7 %copy-start = (bf16[5120,128]{1,0:T(8,128)(2,1)S(1)}, bf16[5120,128]{1,0:T(8,128)(2,1)}, u32[]{:S(2)}) copy-start(bf16[5120,128]{1,0:T(8,128)(2,1)} %param.31) | copy-start | bytes 3932164
  7.2 8.7 copy-start.5
  7.2 158.6 %all-gather.3.cloned.1.call-start = ((), (), s32[]{:S(2)}) async-start(), calls=%async_computation.2 | async-start | bytes 35389440 | tf_op jit(solution)/shard_map/all_gather | solution.py:97
  7.3 7.7 copy-start.2
  15.0 4.4 copy-start.9
  15.0 4.4 copy-start.10
  15.0 4.5 copy-start.7
  15.0 4.5 copy-start.11
  15.0 4.5 copy-start.8
  19.1 679.8 %reduce-scatter.3.cloned.1.call-start = ((), (), s32[]{:S(2)}) async-start(), calls=%async_computation.3 | async-start | bytes 35389440 | tf_op jit(solution)/shard_map/reduce_scatter | solution.py:100
  540.6 0.7 copy-start.6
  540.7 311.3 %all-gather.5.cloned.1.call-start = ((), (), s32[]{:S(2)}) async-start(), calls=%async_computation.4 | async-start | bytes 35389440 | tf_op jit(solution)/shard_map/all_gather | solution.py:103
  698.9 4.8 copy-start.3
  699.0 5.6 copy-start.4
  708.5 701.4 %reduce-scatter.5.cloned.1.call-start = ((), (), s32[]{:S(2)}) async-start(), calls=%async_computation.5 | async-start | bytes 35389440 | tf_op jit(solution)/shard_map/reduce_scatter | solution.py:105
  1251.7 166.6 %copy-start.1 = (bf16[5120,128]{1,0:T(8,128)(2,1)S(1)}, bf16[5120,128]{1,0:T(8,128)(2,1)}, u32[]{:S(2)}) copy-start(bf16[5120,128]{1,0:T(8,128)(2,1)} %param.31) | copy-start | bytes 3932164
Sparse Core Ops, SparseCore 0:
  19.3 146.5 all-gather.2
  540.8 158.1 reduce-scatter.2
  708.6 143.3 all-gather.4
  1251.9 157.9 reduce-scatter.4
where the time goes:
time: 1430 us
  waiting for transfers between devices  595 us (42%)
  matrix products  551 us (39%)
  local copies, waits for them, and re-layouts  110 us (8%)
  other arithmetic  107 us (7%)
  loops' own time  48 us (3%)
    reduce_scatter x1, waiting for transfers between devices, layer(): lax.psum_scatter(down_part, 'tp', scatter_dimension=1, tiled=True)  158 us
    reduce_scatter x1, waiting for transfers between devices, layer(): lax.psum_scatter(attn_part, 'tp', scatter_dimension=1, tiled=True)  158 us
    dot_general x1, matrix products, mlp_partial(): jnp.einsum('rcd,df->rcf', normed_full, w_gate, preferred_element_type=jnp...  150 us
    all_gather x1, waiting for transfers between devices, layer(): mlp_full = lax.all_gather(normed_mlp, 'tp', axis=1, tiled=True)  143 us
    all_gather x1, waiting for transfers between devices, layer(): normed_full = lax.all_gather(normed, 'tp', axis=1, tiled=True)  136 us
    dot_general x1, matrix products, mlp_partial(): jnp.einsum('rcd,df->rcf', normed_full, w_up, preferred_element_type=jnp.f...  126 us
    dot_general x1, matrix products, mlp_partial(): jnp.einsum('rcf,fd->rcd', hidden_act, w_down, preferred_element_type=jnp....  124 us
    dot_general x3, matrix products, project(): jnp.einsum('rcd,dn->rcn', hidden, weight, preferred_element_type=jnp.floa...  62.4 us
  transfers between devices with their start and end apart: 4, of which 4 were waited for; matrix products, arithmetic and copies ran while one was open for 1% of the time, Pallas kernels for 0%

commit v1 on v0

v1 whole, which is shorter than its diff:
```python
import functools

import jax
import jax.numpy as jnp
from jax import lax
from jax.experimental import pallas as pl
from jax.experimental.pallas import tpu as pltpu
from jax.sharding import PartitionSpec as P

ROPE_THETA = 1.0e6
NORM_EPS = 1.0e-6
BF = jnp.bfloat16
F32 = jnp.float32
R = 2
GU = 128
DN = 256
SUB = 16

AT = dict(
    rs1_relay=0.02,
    rs2_half=0.16,
    ag1_fwd=0.26,
    rs1_fin=0.38,
    rs2_relay=0.52,
    ag1_far=0.64,
    ag2_fwd=0.82,
    rs1_half=0.25,
    ag1_own=0.35,
    ag2_fin=0.95,
)


def rope_tables(prefix, n_tokens, head_dim):
    half = head_dim // 2
    inv_freq = ROPE_THETA ** (-(jnp.arange(half, dtype=F32) * 2.0) / head_dim)
    positions = prefix[:, None] + jnp.arange(n_tokens, dtype=jnp.int32)[None, :]
    angles = positions.astype(F32)[..., None] * inv_freq
    cos_t, sin_t = jnp.cos(angles), jnp.sin(angles)
    return jnp.concatenate([cos_t, cos_t], -1), jnp.concatenate([-sin_t, sin_t], -1)


def layer_kernel(
    p_ref, c_ref, bias_ref, g1_ref, g2_ref, x_hbm, cos_hbm, sin_hbm, kc_hbm, vc_hbm, wq_hbm, wk_hbm, wv_hbm, wo_hbm, wg_hbm, wu_hbm, wd_hbm,
    out_hbm, ko_hbm, vo_hbm, h1_hbm, h2_hbm, sb1_hbm, sb2_hbm, rb1_hbm, rb2_hbm, fb1_hbm, fb2_hbm, x1_hbm,
    w_qkv, w_out, gu_buf, dn_buf, h2v, h1v, act, p1, p2, t_a, t_b, t_c, xin, xmid, xend, hb1, hb2, ob, kcv, vcv, kb, vb, kshift, vshift, cosv, sinv, q_buf, o_buf,
    ag_s, ag_r, rs_s, rs_r, tmp_sem, x_sem, h_sem, st_sem, at_sem, kv_sem, gu_sem, dn_sem, w_sem,
):
    n_chunks, blk, width = x_hbm.shape
    half = blk // R
    tokens, hd = cos_hbm.shape[1], cos_hbm.shape[2]
    slots = kc_hbm.shape[1]
    qn = w_out.shape[0]
    ffn = act.shape[1]
    n_gu, n_dn = ffn // GU, width // DN
    n_dev = h1_hbm.shape[1]
    n_chip = n_dev // 2

    me = lax.axis_index("tp")
    core = lax.rem(me, 2)
    chip = lax.div(me, 2)
    chips = [lax.rem(chip + 2, n_chip), lax.rem(chip + 1, n_chip), lax.rem(chip + 3, n_chip), chip]
    far, right_chip, left_chip, _ = chips
    right, left, sib = 2 * right_chip + core, 2 * left_chip + core, me + 1 - 2 * core

    hbufs, gains = (hb1, hb2), (g1_ref, g2_ref)
    h_all, parts = (h1_hbm, h2_hbm), (p1, p2)
    sbs, rbs, fbs = (sb1_hbm, sb2_hbm), (rb1_hbm, rb2_hbm), (fb1_hbm, fb2_hbm)

    def ag(s, c, k):
        h = h_all[s]
        lo, hi = pl.ds(0, half), pl.ds(half, half)
        lt, rt, ft = 2 * left_chip + core, 2 * right_chip + core, 2 * far + core
        own = hbufs[s]
        src, dst, dev = [
            (own, h.at[c, me], right),
            (own, h.at[c, me], left),
            (own, h.at[c, me], sib),
            (h.at[c, lt, lo], h.at[c, lt, lo], right),
            (h.at[c, rt, hi], h.at[c, rt, hi], left),
            (h.at[c, lt], h.at[c, lt], sib),
            (h.at[c, rt], h.at[c, rt], sib),
            (h.at[c, ft, lo], h.at[c, ft, lo], sib),
            (h.at[c, ft, hi], h.at[c, ft, hi], sib),
        ][k]
        return pltpu.make_async_remote_copy(src, dst, ag_s.at[s, c, k], ag_r.at[s, c, k], device_id={"tp": dev})

    def rs(s, c, k):
        p, lo, hi = parts[s], pl.ds(0, half), pl.ds(half, half)
        if k < 4:
            src, dst, dev = p.at[chips[k], 1 - core], sbs[s].at[c, k], sib
        else:
            src, dst, dev = [
                (p.at[far, core, lo], rbs[s].at[c, 0], right),
                (p.at[far, core, hi], rbs[s].at[c, 1], left),
                (p.at[right_chip, core], fbs[s].at[c, 0], right),
                (p.at[left_chip, core], fbs[s].at[c, 1], left),
            ][k - 4]
        return pltpu.make_async_remote_copy(src, dst, rs_s.at[s, c, k], rs_r.at[s, c, k], device_id={"tp": dev})

    def by_rows(rows, fn):
        def step(i, carry):
            fn(pl.ds(pl.multiple_of(i * SUB, SUB), SUB))
            return carry

        lax.fori_loop(0, rows // SUB, step, 0)

    def f32(v):
        return v.astype(F32)

    def normed(wide, gain):
        inv_rms = lax.rsqrt(jnp.mean(wide * wide, axis=-1, keepdims=True) + NORM_EPS)
        return (wide * inv_rms * f32(gain[...])).astype(BF)

    def own_copy(s, c):
        return pltpu.make_async_copy(hbufs[s], h_all[s].at[c, me], h_sem.at[s])

    def x_copy(c):
        return pltpu.make_async_copy(x_hbm.at[c], xin, x_sem.at[0])

    def ag_send(s, c):
        own_copy(s, c).start()
        for k in range(3):
            ag(s, c, k).start()

    def ag1_own(c):
        x_copy(c).wait()

        def fn(rows):
            hb1[rows, :] = normed(f32(xin[rows, :]), g1_ref)

        by_rows(blk, fn)
        ag_send(0, c)

        @pl.when(c + 1 < n_chunks)
        def _():
            x_copy(c + 1).start()

    def ag_fwd(s, c):
        ag(s, c, 0).wait_recv()
        ag(s, c, 3).start()
        ag(s, c, 1).wait_recv()
        ag(s, c, 4).start()
        ag(s, c, 5).start()
        ag(s, c, 6).start()

    def ag_far(s, c):
        for k in (3, 4):
            ag(s, c, k).wait_recv()
            ag(s, c, k + 4).start()

    def ag_fin(s, c):
        for k in (2, 5, 6, 7, 8):
            ag(s, c, k).wait_recv()
        for k in range(9):
            ag(s, c, k).wait_send()
        own_copy(s, c).wait()

    def rs_pair(s, c):
        for k in range(4):
            rs(s, c, k).start()

    def half_loads(s, c):
        return (pltpu.make_async_copy(sbs[s].at[c, 0], t_a, tmp_sem.at[0]),)

    def rs_half_load(s, c):
        rs(s, c, 0).wait_recv()
        for cp in half_loads(s, c):
            cp.start()

    def rs_half(s, c):
        for cp in half_loads(s, c):
            cp.wait()
        p = parts[s]

        def fn(rows):
            p[far, core, rows, :] = (f32(p[far, core, rows, :]) + f32(t_a[rows, :])).astype(BF)

        by_rows(blk, fn)
        rs(s, c, 4).start()
        rs(s, c, 5).start()

    def relay_loads(s, c):
        return (
            pltpu.make_async_copy(sbs[s].at[c, 1], t_a, tmp_sem.at[0]),
            pltpu.make_async_copy(sbs[s].at[c, 2], t_b, tmp_sem.at[1]),
            pltpu.make_async_copy(rbs[s].at[c, 0], t_c.at[pl.ds(0, half)], tmp_sem.at[2]),
            pltpu.make_async_copy(rbs[s].at[c, 1], t_c.at[pl.ds(half, half)], tmp_sem.at[3]),
        )

    def rs_relay_load(s, c):
        loads = relay_loads(s, c)
        for k, cp in zip((1, 2, 4, 5), loads):
            rs(s, c, k).wait_recv()
            cp.start()

    def rs_relay(s, c):
        for cp in relay_loads(s, c):
            cp.wait()
        p = parts[s]

        def first(i):
            lo = pl.ds(pl.multiple_of(i * SUB, SUB), SUB)
            hi = pl.ds(pl.multiple_of(half + i * SUB, SUB), SUB)
            p[right_chip, core, lo, :] = (f32(p[right_chip, core, lo, :]) + f32(t_a[lo, :]) + f32(t_c[lo, :])).astype(BF)
            p[right_chip, core, hi, :] = (f32(p[right_chip, core, hi, :]) + f32(t_a[hi, :])).astype(BF)
            p[left_chip, core, lo, :] = (f32(p[left_chip, core, lo, :]) + f32(t_b[lo, :])).astype(BF)
            p[left_chip, core, hi, :] = (f32(p[left_chip, core, hi, :]) + f32(t_b[hi, :]) + f32(t_c[hi, :])).astype(BF)

        def step(i, carry):
            first(i)
            return carry

        lax.fori_loop(0, half // SUB, step, 0)
        rs(s, c, 6).start()
        rs(s, c, 7).start()

    def fin_loads(s, c):
        return (
            pltpu.make_async_copy(sbs[s].at[c, 3], t_a, tmp_sem.at[0]),
            pltpu.make_async_copy(fbs[s].at[c, 0], t_b, tmp_sem.at[1]),
            pltpu.make_async_copy(fbs[s].at[c, 1], t_c, tmp_sem.at[2]),
        )

    def rs_fin_load(s, c):
        for k, cp in zip((3, 6, 7), fin_loads(s, c)):
            rs(s, c, k).wait_recv()
            cp.start()

    def rs_total(s, rows):
        p = parts[s]
        return (f32(p[chip, core, rows, :]) + f32(t_a[rows, :]) + f32(t_b[rows, :]) + f32(t_c[rows, :])).astype(BF)

    def rs_sent(s, c):
        for k in range(8):
            rs(s, c, k).wait_send()

    def xmid_copy(c):
        return pltpu.make_async_copy(x_hbm.at[c], xmid, x_sem.at[1])

    def x1_store(c):
        return pltpu.make_async_copy(xmid, x1_hbm.at[c], st_sem.at[0])

    def xend_copy(c):
        return pltpu.make_async_copy(x1_hbm.at[c], xend, x_sem.at[2])

    def out_store(c):
        return pltpu.make_async_copy(ob, out_hbm.at[c], st_sem.at[1])

    def rs1_fin(c):
        for cp in fin_loads(0, c):
            cp.wait()
        xmid_copy(c).wait()

        def fn(rows):
            mid = (f32(xmid[rows, :]) + f32(rs_total(0, rows))).astype(BF)
            xmid[rows, :] = mid
            hb2[rows, :] = normed(f32(mid), g2_ref)

        by_rows(blk, fn)
        x1_store(c).start()
        ag_send(1, c)

    def rs2_fin(c):
        rs_fin_load(1, c)
        for cp in fin_loads(1, c):
            cp.wait()
        xend_copy(c).wait()

        def fn(rows):
            ob[rows, :] = (f32(xend[rows, :]) + f32(rs_total(1, rows))).astype(BF)

        by_rows(blk, fn)
        out_store(c).start()
        rs_sent(1, c)

    def att_loads(a, r):
        req = a * R + r
        return (
            pltpu.make_async_copy(h1_hbm.at[a, :, pl.ds(pl.multiple_of(r * half, half), half)], h1v, at_sem.at[0]),
            pltpu.make_async_copy(kc_hbm.at[req], kcv, at_sem.at[1]),
            pltpu.make_async_copy(vc_hbm.at[req], vcv, at_sem.at[2]),
            pltpu.make_async_copy(cos_hbm.at[req], cosv, at_sem.at[3]),
            pltpu.make_async_copy(sin_hbm.at[req], sinv, at_sem.at[4]),
        )

    def attend(a, r):
        req = a * R + r
        for cp in att_loads(a, r):
            cp.wait()
        p, c = p_ref[req], c_ref[req]
        qkv = jnp.dot(h1v[...].reshape(tokens, width), w_qkv[...], preferred_element_type=F32) + f32(bias_ref[...])
        qkv = f32(qkv.astype(BF))
        cos, sin = cosv[...], sinv[...]

        def rope(v):
            return v * cos + pltpu.roll(v, hd // 2, 1) * sin

        for j in range(qn // hd):
            q_buf[:, j * hd : (j + 1) * hd] = rope(qkv[:, j * hd : (j + 1) * hd]).astype(BF)
        kshift[slots : slots + tokens, :] = rope(qkv[:, qn : qn + hd])
        vshift[slots : slots + tokens, :] = qkv[:, qn + hd :]
        slot = lax.broadcasted_iota(jnp.int32, (slots, hd), 0)
        new = (slot >= p) & (slot < p + c)
        kb[...] = jnp.where(new, kshift[pl.ds(slots - p, slots), :], f32(kcv[...])).astype(BF)
        vb[...] = jnp.where(new, vshift[pl.ds(slots - p, slots), :], f32(vcv[...])).astype(BF)
        stores = (pltpu.make_async_copy(kb, ko_hbm.at[req], kv_sem.at[0]), pltpu.make_async_copy(vb, vo_hbm.at[req], kv_sem.at[1]))
        for cp in stores:
            cp.start()

        @pl.when(r + 1 < R)
        def _():
            for cp in att_loads(a, r + 1):
                cp.start()

        limit = p + jnp.minimum(lax.broadcasted_iota(jnp.int32, (tokens, slots), 0), c - 1)
        visible = lax.broadcasted_iota(jnp.int32, (tokens, slots), 1) <= limit
        for j in range(qn // hd):
            cols = slice(j * hd, (j + 1) * hd)
            scores = lax.dot_general(q_buf[:, cols], kb[...], (((1,), (1,)), ((), ())), preferred_element_type=F32) * (hd**-0.5)
            scores = jnp.where(visible, scores, -1.0e30)
            expd = jnp.exp(scores - jnp.max(scores, axis=1, keepdims=True))
            probs = (expd * (1.0 / jnp.sum(expd, axis=1, keepdims=True))).astype(BF)
            o_buf[:, cols] = jnp.dot(probs, vb[...], preferred_element_type=F32).astype(BF)

        def out_tile(i, carry):
            cols = pl.ds(pl.multiple_of(i * 2 * DN, 2 * DN), 2 * DN)
            tile = jnp.dot(o_buf[...], w_out[:, cols], preferred_element_type=F32).astype(BF)
            p1[:, :, pl.ds(pl.multiple_of(r * half, half), half), cols] = tile.reshape(n_chip, 2, half, 2 * DN)
            return carry

        lax.fori_loop(0, width // (2 * DN), out_tile, 0)
        for cp in stores:
            cp.wait()

    def gu_copies(tile, slot):
        cols = pl.ds(pl.multiple_of(tile * GU, GU), GU)
        return (
            pltpu.make_async_copy(wg_hbm.at[:, cols], gu_buf.at[slot, :, pl.ds(0, GU)], gu_sem.at[slot, 0]),
            pltpu.make_async_copy(wu_hbm.at[:, cols], gu_buf.at[slot, :, pl.ds(GU, GU)], gu_sem.at[slot, 1]),
        )

    def dn_copy(tile, slot):
        cols = pl.ds(pl.multiple_of(tile * DN, DN), DN)
        return pltpu.make_async_copy(wd_hbm.at[:, cols], dn_buf.at[slot], dn_sem.at[slot])

    def h2_load(c):
        return pltpu.make_async_copy(h2_hbm.at[c], h2v, h_sem.at[2])

    def qkv_loads():
        return (
            pltpu.make_async_copy(wq_hbm, w_qkv.at[:, pl.ds(0, qn)], w_sem.at[0]),
            pltpu.make_async_copy(wk_hbm, w_qkv.at[:, pl.ds(qn, hd)], w_sem.at[1]),
            pltpu.make_async_copy(wv_hbm, w_qkv.at[:, pl.ds(qn + hd, hd)], w_sem.at[2]),
            pltpu.make_async_copy(wo_hbm, w_out, w_sem.at[3]),
        )

    x_copy(0).start()
    barrier = pltpu.get_barrier_semaphore()
    for dev in (right, left, sib):
        pl.semaphore_signal(barrier, inc=1, device_id={"tp": dev})
    pl.semaphore_wait(barrier, 3)
    ag1_own(0)
    for cp in qkv_loads():
        cp.start()
    for cp in gu_copies(0, 0):
        cp.start()
    kshift[...] = jnp.zeros_like(kshift)
    vshift[...] = jnp.zeros_like(vshift)
    for cp in qkv_loads():
        cp.wait()

    def ok(c):
        return (c >= 0) & (c < n_chunks)

    def step(t, carry):
        mlp, mid, old = t - 2, t - 1, t - 3

        def event(now, name, phase, chunk, fn, late=0):
            at = min(int(AT[name] * phase) + late, phase - 1)

            @pl.when((now == at) & ok(chunk))
            def _():
                fn(chunk)

        def relay1_load(c):
            xmid_copy(c).start()
            rs_relay_load(0, c)

        def relay2_load(c):
            xend_copy(c).start()
            rs_relay_load(1, c)

        def gu_step(j, carry):
            event(j, "rs1_relay", n_gu, mid, relay1_load)
            event(j, "rs1_relay", n_gu, mid, lambda c: rs_relay(0, c), 1)
            event(j, "rs2_half", n_gu, old, lambda c: rs_half_load(1, c))
            event(j, "rs2_half", n_gu, old, lambda c: rs_half(1, c), 1)
            event(j, "ag1_fwd", n_gu, t, lambda c: ag_fwd(0, c))
            event(j, "rs1_fin", n_gu, mid, lambda c: rs_fin_load(0, c))
            event(j, "rs1_fin", n_gu, mid, rs1_fin, 1)
            event(j, "rs2_relay", n_gu, old, relay2_load)
            event(j, "rs2_relay", n_gu, old, lambda c: rs_relay(1, c), 1)
            event(j, "ag1_far", n_gu, t, lambda c: ag_far(0, c))
            event(j, "ag2_fwd", n_gu, mid, lambda c: ag_fwd(1, c))

            @pl.when(ok(mlp))
            def _():
                slot = lax.rem(j, 2)

                @pl.when(j == 0)
                def _():
                    dn_copy(0, 0).start()
                    h2_load(mlp).wait()

                @pl.when(j + 1 < n_gu)
                def _():
                    for cp in gu_copies(j + 1, 1 - slot):
                        cp.start()

                for cp in gu_copies(j, slot):
                    cp.wait()
                both = jnp.dot(h2v[...].reshape(n_dev * blk, width), gu_buf[slot], preferred_element_type=F32)
                gate, up = both[:, :GU], both[:, GU:]
                act[:, pl.ds(pl.multiple_of(j * GU, GU), GU)] = (jax.nn.silu(gate) * up).astype(BF)

            return carry

        lax.fori_loop(0, n_gu, gu_step, 0)

        @pl.when(ok(mlp) & (mlp + 1 < n_chunks))
        def _():
            for cp in gu_copies(0, 0):
                cp.start()

        @pl.when(ok(mid))
        def _():
            rs_sent(0, mid)
            x1_store(mid).wait()

        @pl.when(ok(t))
        def _():
            ag_fin(0, t)
            for cp in att_loads(t, 0):
                cp.start()

        @pl.when(ok(old))
        def _():
            rs2_fin(old)

        def att_step(r, carry):
            @pl.when(ok(t))
            def _():
                attend(t, r)

            @pl.when((r == 0) & ok(mid))
            def _():
                ag_far(1, mid)

            return carry

        lax.fori_loop(0, R, att_step, 0)

        @pl.when(ok(t))
        def _():
            rs_pair(0, t)

        def dn_step(j, carry):
            event(j, "rs1_half", n_dn, t, lambda c: rs_half_load(0, c))
            event(j, "rs1_half", n_dn, t, lambda c: rs_half(0, c), 1)
            event(j, "ag1_own", n_dn, t + 1, ag1_own)

            def fin2(c):
                ag_fin(1, c)
                h2_load(c).start()

            event(j, "ag2_fin", n_dn, mid, fin2)

            @pl.when(ok(mlp))
            def _():
                slot = lax.rem(j, 2)

                @pl.when(j + 1 < n_dn)
                def _():
                    dn_copy(j + 1, 1 - slot).start()

                dn_copy(j, slot).wait()
                tile = jnp.dot(act[...], dn_buf[slot], preferred_element_type=F32).astype(BF)
                p2[:, :, :, pl.ds(pl.multiple_of(j * DN, DN), DN)] = tile.reshape(n_chip, 2, blk, DN)

            return carry

        lax.fori_loop(0, n_dn, dn_step, 0)

        @pl.when(ok(old))
        def _():
            out_store(old).wait()

        @pl.when(ok(mlp))
        def _():
            rs_pair(1, mlp)

        return carry

    lax.fori_loop(0, n_chunks + 3, step, 0)


def fused_layer(x, cos, sin, bias, k_cache, v_cache, prefix, valid, g_attn, g_mlp, w_q, w_k, w_v, w_o, w_gate, w_up, w_down, n_dev):
    n_req, rows, width = x.shape
    n_chunks, blk = n_req // R, R * rows
    slots, hd = k_cache.shape[1:]
    tokens, qn, ffn = n_dev * rows, w_q.shape[1], w_gate.shape[1]
    n_chip = n_dev // 2
    hbm, smem, vmem = (pl.BlockSpec(memory_space=m) for m in (pl.ANY, pltpu.SMEM, pltpu.VMEM))
    chunked = lambda *s: jax.ShapeDtypeStruct((n_chunks, *s, width), BF)
    out_shape = [
        chunked(blk),
        jax.ShapeDtypeStruct(k_cache.shape, BF),
        jax.ShapeDtypeStruct(v_cache.shape, BF),
        chunked(n_dev, blk),
        chunked(n_dev, blk),
        chunked(n_chip, blk),
        chunked(n_chip, blk),
        chunked(2, rows),
        chunked(2, rows),
        chunked(2, blk),
        chunked(2, blk),
        chunked(blk),
    ]
    dma = lambda *s: pltpu.SemaphoreType.DMA(s)
    rows_buf = pltpu.VMEM((blk, width), BF)
    scratch = [
        pltpu.VMEM((width, qn + 2 * hd), BF),
        pltpu.VMEM((qn, width), BF),
        pltpu.VMEM((2, width, 2 * GU), BF),
        pltpu.VMEM((2, ffn, DN), BF),
        pltpu.VMEM((n_dev, blk, width), BF),
        pltpu.VMEM((n_dev, rows, width), BF),
        pltpu.VMEM((n_dev * blk, ffn), BF),
        pltpu.VMEM((n_chip, 2, blk, width), BF),
        pltpu.VMEM((n_chip, 2, blk, width), BF),
        *[rows_buf] * 9,
        *[pltpu.VMEM((slots, hd), BF)] * 4,
        *[pltpu.VMEM((2 * slots, hd), F32)] * 2,
        *[pltpu.VMEM((tokens, hd), F32)] * 2,
        *[pltpu.VMEM((tokens, qn), BF)] * 2,
        dma(2, n_chunks, 9),
        dma(2, n_chunks, 9),
        dma(2, n_chunks, 8),
        dma(2, n_chunks, 8),
        dma(4),
        dma(3),
        dma(3),
        dma(2),
        dma(5),
        dma(2),
        dma(2, 2),
        dma(2),
        dma(4),
    ]
    res = pl.pallas_call(
        layer_kernel,
        in_specs=[smem, smem, vmem, vmem, vmem] + [hbm] * 12,
        out_specs=[hbm] * len(out_shape),
        out_shape=out_shape,
        scratch_shapes=scratch,
        compiler_params=pltpu.CompilerParams(vmem_limit_bytes=67_000_000, collective_id=0, has_side_effects=True),
        name="layer",
    )(prefix, valid, bias, g_attn[None], g_mlp[None], x.reshape(n_chunks, blk, width), cos, sin, k_cache, v_cache, w_q, w_k, w_v, w_o, w_gate, w_up, w_down)
    return res[0].reshape(x.shape), res[1], res[2]


def solution(mesh):
    row_spec = P("dp", "tp", None)
    cache_spec = P("dp", None, "tp", None)
    req_spec = P("dp")
    rep_spec = P(None)
    col_spec = P(None, "tp")
    bias_spec = P("tp")
    down_spec = P("tp", None)
    n_dev = mesh.shape["tp"]

    def layer(x_rows, k_cache, v_cache, prefix, valid, g_attn, w_q, b_q, w_k, b_k, w_v, b_v, w_o, g_mlp, w_gate, w_up, w_down):
        n_req, rows, _ = x_rows.shape
        slots, hd = k_cache.shape[1], k_cache.shape[3]
        keys, vals = k_cache.reshape(n_req, slots, hd), v_cache.reshape(n_req, slots, hd)
        cos, sin = rope_tables(prefix, rows * n_dev, hd)
        bias = jnp.concatenate([b_q, b_k, b_v])[None]
        out, k_out, v_out = fused_layer(x_rows, cos, sin, bias, keys, vals, prefix, valid, g_attn, g_mlp, w_q, w_k, w_v, w_o, w_gate, w_up, w_down, n_dev)
        return out, k_out.reshape(k_cache.shape), v_out.reshape(v_cache.shape)

    in_specs = (row_spec, cache_spec, cache_spec, req_spec, req_spec, rep_spec, col_spec, bias_spec, col_spec, bias_spec, col_spec, bias_spec, down_spec, rep_spec, col_spec, col_spec, down_spec)
    return jax.shard_map(layer, mesh=mesh, in_specs=in_specs, out_specs=(row_spec, cache_spec, cache_spec), check_vma=False)
```

time: 1430 us -> 826 us (0.58)
  Pallas kernels: 0 us -> 796 us
  waiting for transfers between devices: 595 us -> 0 us
  matrix products: 551 us -> 0 us
  local copies, waits for them, and re-layouts: 110 us -> 12.4 us
  other arithmetic: 107 us -> 9.65 us
  loops' own time: 48 us -> 0 us
    pallas_call x0 -> x1, Pallas kernels: none -> 796 us  [fused_layer(): pl.pallas_call(layer_kernel, in_specs=[smem, smem, vmem, vmem, vmem] + [h...]
    dot_general x9 -> x0, matrix products: 551 us -> none  [the longest x1 150 us: mlp_partial(): jnp.einsum('rcd,df->rcf', normed_full, w_gate, preferred_element_type=jnp...]
    reduce_scatter x2 -> x0, waiting for transfers between devices: 316 us -> none  [the longest x1 158 us: layer(): lax.psum_scatter(down_part, 'tp', scatter_dimension=1, tiled=True)]
    all_gather x2 -> x0, waiting for transfers between devices: 279 us -> none  [the longest x1 143 us: layer(): mlp_full = lax.all_gather(normed_mlp, 'tp', axis=1, tiled=True)]
    another operation x2 -> x0, loops' own time: 48 us -> none  [write_rows(): return lax.fori_loop(0, cache.shape[0], body, cache)]
    dynamic_update_slice x24 -> x0, local copies, waits for them, and re-layouts: 38.1 us -> none  [body(): return lax.dynamic_update_slice(buffer, merged, (req_idx, start, 0, 0))]
    dynamic_slice x72 -> x0, local copies, waits for them, and re-layouts: 32.6 us -> none  [the longest x24 15.6 us: body(): merged = jnp.where(row_ids < valid[req_idx], fresh, old_rows)]
    reduce_sum x3 -> x0, other arithmetic: 26.9 us -> none  [the longest x1 21.2 us: attend(): attn_probs = jax.nn.softmax(scores, axis=-1).astype(jnp.bfloat16)]
  transfers between devices with their start and end apart: 4 -> 0, of which waited for: 4 -> 0; matrix products, arithmetic and copies ran while one was open for 1% -> 0% of each run, Pallas kernels for 0% -> 0%
where the time goes in v1:
time: 826 us; the launch traced here: 818 us
  Pallas kernels  796 us (96%)
  local copies, waits for them, and re-layouts  12.4 us (2%)
  other arithmetic  9.65 us (1%)
    pallas_call x1, Pallas kernels, fused_layer(): pl.pallas_call(layer_kernel, in_specs=[smem, smem, vmem, vmem, vmem] + [h...  796 us

profile of v1, /device:TPU:112, one launch (start us, length us, event | category | flops | bytes accessed | tf_op | source)
XLA Modules:
  0.0 818.5 jit_solution(9752951542777812248)
XLA Ops:
  0.6 0.7 pad_maximum_fusion.2
  1.4 0.6 broadcast_in_dim.6.bias_ref
  2.0 0.7 add_convert_fusion
  2.7 1.3 broadcast_in_dim.14.g1_ref
  4.0 1.3 broadcast_in_dim.15.g2_ref
  5.3 5.6 fusion
  11.0 2.5 pad_maximum_fusion
  13.5 795.8 %layer.1 = (bf16[6,64,5120]{2,1,0:T(8,128)(2,1)}, bf16[12,1024,128]{2,1,0:T(8,128)(2,1)}, bf16[12,1024,128]{2,1,0:T(8,128)(2,1)}, bf16[6,8,64,5120]{3,2,1,0:T(8,...) custom-call(s32[12]{0:T(128)} %p_ref.1, s32[12]{0:T(128)} %c_ref.1, ...), custom_call_target="tpu_custom_call" | custom-call | tf_op jit(solution)/shard_map/layer/pallas_call | solution.py:560
  809.3 0.0 copy-start.1
  809.3 4.4 copy.25
  813.8 0.0 copy-done.1
  813.8 0.0 copy-start
  813.8 1.7 copy.26
  815.4 1.4 copy-done
  816.8 1.7 copy.27
  (1 shorter events, 0.0 us)
Async XLA Ops:
  809.3 4.5 copy-start.1
  813.8 3.0 copy-start

commit v2 on v1

v2 whole, which is shorter than its diff:
```python
import jax
import jax.numpy as jnp
import numpy as np
from jax import lax
from jax.experimental import pallas as pl
from jax.experimental.pallas import tpu as pltpu
from jax.sharding import PartitionSpec as P

ROPE_THETA = 1.0e6
NORM_EPS = 1.0e-6
LOG2_E = 1.4426950408889634
BF = jnp.bfloat16
F32 = jnp.float32
R = 2
GU = 384
DN = 512
GU_SLOTS, DN_SLOTS = 2, 2
QA = 512
SUB = 16
LEAD = 3

GU_PARTS, DN_PARTS = 9, 5


def layer_kernel(
    p_ref, c_ref, bias_ref, g1_ref, g2_ref, freq_ref, x_hbm, kc_hbm, vc_hbm, wq_hbm, wk_hbm, wv_hbm, wo_hbm, wg_hbm, wu_hbm, wd_hbm,
    out_hbm, ko_hbm, vo_hbm, h1_hbm, h2_hbm, sb1_hbm, sb2_hbm, rb1_hbm, rb2_hbm, fb1_hbm, fb2_hbm, x1_hbm, cs_hbm,
    w_out, gu_buf, dn_buf, h2v, h1v, act, pp, t_a, t_b, t_c, xin, xmid, xend, hb1, hb2, kb, vb, shift, csv, sbuf,
    ag_s, ag_r, rs_s, rs_r, tmp_sem, x_sem, h_sem, st_sem, at_sem, kv_sem, gu_sem, dn_sem, w_sem, h2_sem,
):
    n_chunks, blk, width = x_hbm.shape
    half = blk // R
    tokens, hd = cs_hbm.shape[1], cs_hbm.shape[2]
    slots = kc_hbm.shape[1]
    qn = w_out.shape[0]
    ffn = act.shape[1]
    n_gu, n_dn = ffn // GU, width // DN
    n_dev = h1_hbm.shape[1]
    n_chip = n_dev // 2

    me = lax.axis_index("tp")
    core = lax.rem(me, 2)
    chip = lax.div(me, 2)
    chips = [lax.rem(chip + 2, n_chip), lax.rem(chip + 1, n_chip), lax.rem(chip + 3, n_chip), chip]
    far, right_chip, left_chip, _ = chips
    right, left, sib = 2 * right_chip + core, 2 * left_chip + core, me + 1 - 2 * core

    hbufs, gains = (hb1, hb2), (g1_ref, g2_ref)
    h_all = (h1_hbm, h2_hbm)
    sbs, rbs, fbs = (sb1_hbm, sb2_hbm), (rb1_hbm, rb2_hbm), (fb1_hbm, fb2_hbm)

    def part(s, c):
        return pp.at[1 if s else jnp.where(c == 1, 1, 0)]

    def h_slot(s, c):
        return 0 if s else lax.rem(c, 2)

    def ag(s, c, k):
        h = h_all[s]
        lo, hi = pl.ds(0, half), pl.ds(half, half)
        lt, rt, ft = 2 * left_chip + core, 2 * right_chip + core, 2 * far + core
        own = hbufs[s].at[h_slot(s, c)]
        src, dst, dev = [
            (own, h.at[c, me], right),
            (own, h.at[c, me], left),
            (own, h.at[c, me], sib),
            (h.at[c, lt, lo], h.at[c, lt, lo], right),
            (h.at[c, rt, hi], h.at[c, rt, hi], left),
            (h.at[c, lt], h.at[c, lt], sib),
            (h.at[c, rt], h.at[c, rt], sib),
            (h.at[c, ft, lo], h.at[c, ft, lo], sib),
            (h.at[c, ft, hi], h.at[c, ft, hi], sib),
        ][k]
        return pltpu.make_async_remote_copy(src, dst, ag_s.at[s, c, k], ag_r.at[s, c, k], device_id={"tp": dev})

    def rs(s, c, k, cut=None):
        col, row = (pl.ds(0, width), c) if cut is None else (pl.ds(*cut[:2]), n_chunks - 1 + cut[2])
        p, lo, hi = part(s, c), pl.ds(0, half), pl.ds(half, half)
        all_rows = pl.ds(0, blk)
        if k < 4:
            src, dst, dev = p.at[chips[k], 1 - core, all_rows, col], sbs[s].at[c, k, all_rows, col], sib
        else:
            src, dst, dev = [
                (p.at[far, core, lo, col], rbs[s].at[c, 0, pl.ds(0, half), col], right),
                (p.at[far, core, hi, col], rbs[s].at[c, 1, pl.ds(0, half), col], left),
                (p.at[right_chip, core, all_rows, col], fbs[s].at[c, 0, all_rows, col], right),
                (p.at[left_chip, core, all_rows, col], fbs[s].at[c, 1, all_rows, col], left),
            ][k - 4]
        return pltpu.make_async_remote_copy(src, dst, rs_s.at[s, row, k], rs_r.at[s, row, k], device_id={"tp": dev})

    def by_rows(rows, fn):
        def step(i, carry):
            fn(pl.ds(pl.multiple_of(i * SUB, SUB), SUB))
            return carry

        lax.fori_loop(0, rows // SUB, step, 0)

    def f32(v):
        return v.astype(F32)

    def normed(wide, gain):
        inv_rms = lax.rsqrt(jnp.mean(wide * wide, axis=-1, keepdims=True) + NORM_EPS)
        return (wide * inv_rms * f32(gain[...])).astype(BF)

    def own_copy(s, c):
        slot = h_slot(s, c)
        return pltpu.make_async_copy(hbufs[s].at[slot], h_all[s].at[c, me], h_sem.at[s, slot])

    def x_copy(c):
        return pltpu.make_async_copy(x_hbm.at[c], xin, x_sem.at[0])

    def ag_send(s, c):
        own_copy(s, c).start()
        for k in range(3):
            ag(s, c, k).start()

    def ag1_own(c):
        x_copy(c).wait()

        def fn(rows):
            hb1[h_slot(0, c), rows, :] = normed(f32(xin[rows, :]), g1_ref)

        by_rows(blk, fn)
        ag_send(0, c)

        @pl.when(c + 1 < n_chunks)
        def _():
            x_copy(c + 1).start()

    def ag_fwd(s, c):
        ag(s, c, 0).wait_recv()
        ag(s, c, 3).start()
        ag(s, c, 1).wait_recv()
        ag(s, c, 4).start()
        ag(s, c, 5).start()
        ag(s, c, 6).start()

    def ag_far(s, c):
        for k in (3, 4):
            ag(s, c, k).wait_recv()
            ag(s, c, k + 4).start()

    def ag_fin(s, c):
        for k in (2, 5, 6, 7, 8):
            ag(s, c, k).wait_recv()
        for k in range(9):
            ag(s, c, k).wait_send()
        own_copy(s, c).wait()

    def rs_pair(s, c, cut=None):
        for k in range(4):
            rs(s, c, k, cut).start()

    def loads(srcs, cut):
        col = pl.ds(0, width) if cut is None else pl.ds(*cut[:2])
        return [
            pltpu.make_async_copy(src.at[:, col], dst.at[:, col], tmp_sem.at[i]) for i, (src, dst) in enumerate(srcs)
        ]

    def half_loads(s, c, cut):
        return loads([(sbs[s].at[c, 0], t_a)], cut)

    def rs_half_load(s, c, cut=None):
        rs(s, c, 0, cut).wait_recv()
        for cp in half_loads(s, c, cut):
            cp.start()

    def rs_half(s, c, cut=None):
        for cp in half_loads(s, c, cut):
            cp.wait()
        p, col = part(s, c), slice(None) if cut is None else pl.ds(*cut[:2])

        def fn(rows):
            p[far, core, rows, col] = (f32(p[far, core, rows, col]) + f32(t_a[rows, col])).astype(BF)

        by_rows(blk, fn)
        rs(s, c, 4, cut).start()
        rs(s, c, 5, cut).start()

    def relay_loads(s, c, cut):
        lo, hi = t_c.at[pl.ds(0, half)], t_c.at[pl.ds(half, half)]
        return loads([(sbs[s].at[c, 1], t_a), (sbs[s].at[c, 2], t_b), (rbs[s].at[c, 0], lo), (rbs[s].at[c, 1], hi)], cut)

    def rs_relay_load(s, c, cut=None):
        for k, cp in zip((1, 2, 4, 5), relay_loads(s, c, cut)):
            rs(s, c, k, cut).wait_recv()
            cp.start()

    def rs_relay(s, c, cut=None):
        for cp in relay_loads(s, c, cut):
            cp.wait()
        p, col = part(s, c), slice(None) if cut is None else pl.ds(*cut[:2])

        def step(i, carry):
            lo = pl.ds(pl.multiple_of(i * SUB, SUB), SUB)
            hi = pl.ds(pl.multiple_of(half + i * SUB, SUB), SUB)
            p[right_chip, core, lo, col] = (f32(p[right_chip, core, lo, col]) + f32(t_a[lo, col]) + f32(t_c[lo, col])).astype(BF)
            p[right_chip, core, hi, col] = (f32(p[right_chip, core, hi, col]) + f32(t_a[hi, col])).astype(BF)
            p[left_chip, core, lo, col] = (f32(p[left_chip, core, lo, col]) + f32(t_b[lo, col])).astype(BF)
            p[left_chip, core, hi, col] = (f32(p[left_chip, core, hi, col]) + f32(t_b[hi, col]) + f32(t_c[hi, col])).astype(BF)
            return carry

        lax.fori_loop(0, half // SUB, step, 0)
        rs(s, c, 6, cut).start()
        rs(s, c, 7, cut).start()

    def fin_loads(s, c, cut):
        return loads([(sbs[s].at[c, 3], t_a), (fbs[s].at[c, 0], t_b), (fbs[s].at[c, 1], t_c)], cut)

    def rs_fin_load(s, c, cut=None):
        for k, cp in zip((3, 6, 7), fin_loads(s, c, cut)):
            rs(s, c, k, cut).wait_recv()
            cp.start()

    def rs_total(s, c, rows, col=slice(None)):
        p = part(s, c)
        return (f32(p[chip, core, rows, col]) + f32(t_a[rows, col]) + f32(t_b[rows, col]) + f32(t_c[rows, col])).astype(BF)

    def rs_sent(s, c, cut=None):
        for k in range(8):
            rs(s, c, k, cut).wait_send()

    def xmid_copy(c):
        return pltpu.make_async_copy(x_hbm.at[c], xmid, x_sem.at[1])

    def x1_store(c):
        return pltpu.make_async_copy(xmid, x1_hbm.at[c], st_sem.at[0])

    def xend_copy(c):
        return pltpu.make_async_copy(x1_hbm.at[c], xend, x_sem.at[2])

    def out_store(c):
        return pltpu.make_async_copy(xend, out_hbm.at[c], st_sem.at[1])

    def rs1_fin_load(c):
        @pl.when(c > 0)
        def _():
            x1_store(c - 1).wait()

        xmid_copy(c).start()
        rs_fin_load(0, c)

    def rs1_fin(c):
        for cp in fin_loads(0, c, None):
            cp.wait()
        xmid_copy(c).wait()

        def fn(rows):
            mid = (f32(xmid[rows, :]) + f32(rs_total(0, c, rows))).astype(BF)
            xmid[rows, :] = mid
            hb2[0, rows, :] = normed(f32(mid), g2_ref)

        by_rows(blk, fn)
        x1_store(c).start()
        ag_send(1, c)

    def rs2_fin_load(c):
        @pl.when(c > 0)
        def _():
            out_store(c - 1).wait()

        xend_copy(c).start()
        rs_fin_load(1, c)

    def rs2_add(c, cut=None):
        for cp in fin_loads(1, c, cut):
            cp.wait()
        col = slice(None) if cut is None else pl.ds(*cut[:2])

        def fn(rows):
            xend[rows, col] = (f32(xend[rows, col]) + f32(rs_total(1, c, rows, col))).astype(BF)

        by_rows(blk, fn)

    def rs2_fin(c):
        xend_copy(c).wait()
        rs2_add(c)
        out_store(c).start()
        rs_sent(1, c)

    def att_loads(a, r):
        return (
            pltpu.make_async_copy(h1_hbm.at[a, :, pl.ds(pl.multiple_of(r * half, half), half)], h1v, at_sem.at[0]),
            pltpu.make_async_copy(cs_hbm.at[a * R + r], csv, at_sem.at[3]),
        )

    def cache_loads(a, r):
        return (
            pltpu.make_async_copy(kc_hbm.at[a * R + r], kb, at_sem.at[1]),
            pltpu.make_async_copy(vc_hbm.at[a * R + r], vb, at_sem.at[2]),
        )

    def table(req, carry):
        pos = p_ref[req] + lax.broadcasted_iota(jnp.int32, (tokens, hd), 0)
        angles = f32(pos) * freq_ref[...]
        first = lax.broadcasted_iota(jnp.int32, (tokens, hd), 1) < hd // 2
        csv[...] = jnp.where(first, jnp.cos(angles), jnp.sin(angles))
        cp = pltpu.make_async_copy(csv, cs_hbm.at[req], at_sem.at[3])
        cp.start()
        cp.wait()
        return carry

    def attend(a, r):
        req = a * R + r
        p_out = part(0, a)
        for cp in (*att_loads(a, r), *cache_loads(a, r)):
            cp.wait()
        fresh = (r == 0) & ((a == 0) | (a >= LEAD))
        h = h1v[...].reshape(tokens, width)

        def project(cps, slot, lo, size):
            @pl.when(fresh)
            def _():
                for cp in cps:
                    cp.wait()

            total = jnp.dot(h, gu_buf[slot, :, 0:size], preferred_element_type=F32)
            return f32((total + f32(bias_ref[:, lo : lo + size])).astype(BF))

        some_q = project(qa_loads(), 1, 0, QA)
        rest = project(qb_loads(), 0, QA, qn + 2 * hd - QA)
        p, c = p_ref[req], c_ref[req]
        cs = csv[...]
        sc = pltpu.roll(cs, hd // 2, 1)
        first = lax.broadcasted_iota(jnp.int32, (tokens, hd), 1) < hd // 2
        cos, sin = jnp.where(first, cs, sc), jnp.where(first, -sc, cs)

        def head(j):
            return some_q[:, j * hd : (j + 1) * hd] if j * hd < QA else rest[:, j * hd - QA : (j + 1) * hd - QA]

        def rope(v):
            return v * cos + pltpu.roll(v, hd // 2, 1) * sin

        n_heads, groups = qn // hd, tokens // blk
        for j in range(n_heads):
            h2v[0:groups, :, j * hd : (j + 1) * hd] = rope(head(j)).astype(BF).reshape(groups, blk, hd)
        slot = lax.broadcasted_iota(jnp.int32, (slots, hd), 0)
        new = (slot >= p) & (slot < p + c)
        shift[slots : slots + tokens, :] = rope(head(n_heads))
        kb[...] = jnp.where(new, shift[pl.ds(slots - p, slots), :], f32(kb[...])).astype(BF)
        shift[slots : slots + tokens, :] = head(n_heads + 1)
        vb[...] = jnp.where(new, shift[pl.ds(slots - p, slots), :], f32(vb[...])).astype(BF)
        stores = (pltpu.make_async_copy(kb, ko_hbm.at[req], kv_sem.at[0]), pltpu.make_async_copy(vb, vo_hbm.at[req], kv_sem.at[1]))
        for cp in stores:
            cp.start()

        @pl.when(r + 1 < R)
        def _():
            for cp in att_loads(a, r + 1):
                cp.start()

        @pl.when((r == R - 1) & (a >= LEAD - 1))
        def _():
            start_gu()

        def scores(j):
            q = h2v[0:groups, :, j * hd : (j + 1) * hd].reshape(tokens, hd)
            return lax.dot_general(q, kb[...], (((1,), (1,)), ((), ())), preferred_element_type=F32)

        limit = p + jnp.minimum(lax.broadcasted_iota(jnp.int32, (tokens, slots), 0), c - 1)
        visible = lax.broadcasted_iota(jnp.int32, (tokens, slots), 1) <= limit
        sbuf[0] = scores(0)
        for j in range(n_heads):
            if j + 1 < n_heads:
                sbuf[(j + 1) % 2] = scores(j + 1)
            masked = jnp.where(visible, sbuf[j % 2], -1.0e30)
            expd = jnp.exp2((masked - jnp.max(masked, axis=1, keepdims=True)) * (hd**-0.5 * LOG2_E))
            probs = (expd * (1.0 / jnp.sum(expd, axis=1, keepdims=True))).astype(BF)
            mixed = jnp.dot(probs, vb[...], preferred_element_type=F32).astype(BF)
            h2v[groups : 2 * groups, :, j * hd : (j + 1) * hd] = mixed.reshape(groups, blk, hd)
        for cp in stores:
            cp.wait()

        @pl.when(r + 1 < R)
        def _():
            for cp in cache_loads(a, r + 1):
                cp.start()

        heads = h2v[groups : 2 * groups, :, 0:qn].reshape(tokens, qn)
        out = jnp.dot(heads, w_out[...], preferred_element_type=F32).astype(BF)
        p_out[:, :, pl.ds(pl.multiple_of(r * half, half), half), :] = out.reshape(n_chip, 2, half, width)

    def gu_copies(tile, slot):
        cols = pl.ds(pl.multiple_of(tile * GU, GU), GU)
        return (
            pltpu.make_async_copy(wg_hbm.at[:, cols], gu_buf.at[slot, :, pl.ds(0, GU)], gu_sem.at[slot, 0]),
            pltpu.make_async_copy(wu_hbm.at[:, cols], gu_buf.at[slot, :, pl.ds(GU, GU)], gu_sem.at[slot, 1]),
        )

    def dn_copy(tile, slot):
        cols = pl.ds(pl.multiple_of(tile * DN, DN), DN)
        return pltpu.make_async_copy(wd_hbm.at[:, cols], dn_buf.at[slot], dn_sem.at[slot])

    def h2_load(c):
        return pltpu.make_async_copy(h2_hbm.at[c], h2v, h2_sem)

    def start_gu():
        for tile in range(GU_SLOTS - 1):
            for cp in gu_copies(tile, tile):
                cp.start()

    def qa_loads():
        return (pltpu.make_async_copy(wq_hbm.at[:, pl.ds(0, QA)], gu_buf.at[1, :, pl.ds(0, QA)], w_sem.at[0]),)

    def qb_loads():
        left_q = qn - QA
        return (
            pltpu.make_async_copy(wq_hbm.at[:, pl.ds(QA, left_q)], gu_buf.at[0, :, pl.ds(0, left_q)], w_sem.at[1]),
            pltpu.make_async_copy(wk_hbm, gu_buf.at[0, :, pl.ds(left_q, hd)], w_sem.at[2]),
            pltpu.make_async_copy(wv_hbm, gu_buf.at[0, :, pl.ds(left_q + hd, hd)], w_sem.at[3]),
        )

    x_copy(0).start()
    barrier = pltpu.get_barrier_semaphore()
    for dev in (right, left, sib):
        pl.semaphore_signal(barrier, inc=1, device_id={"tp": dev})
    pl.semaphore_wait(barrier, 3)
    ag1_own(0)
    wo_copy = pltpu.make_async_copy(wo_hbm, w_out, w_sem.at[4])
    for cp in (*qa_loads(), *qb_loads(), wo_copy):
        cp.start()
    shift[...] = jnp.zeros_like(shift)
    lax.fori_loop(0, n_chunks * R, table, 0)
    wo_copy.wait()

    def ready(c):
        ag_fin(0, c)
        for cp in (*att_loads(c, 0), *cache_loads(c, 0)):
            cp.start()

    def lead(i, carry):
        @pl.when(i == 0)
        def _():
            ag_fwd(0, 0)
            ag1_own(1)
            ag_far(0, 0)
            ready(0)

        @pl.when(i == 1)
        def _():
            ag_fwd(0, 1)
            ag1_own(2)

        @pl.when(i == R)
        def _():
            ag_far(0, 1)
            rs_pair(0, 0)
            ready(1)
            rs_half_load(0, 0)
            rs_half(0, 0)

        @pl.when(i == R + 1)
        def _():
            ag_fwd(0, 2)
            rs_relay_load(0, 0)
            rs_relay(0, 0)

        @pl.when(i == 2 * R)
        def _():
            ag_far(0, 2)
            rs_pair(0, 1)
            rs1_fin_load(0)
            rs1_fin(0)
            ready(2)
            rs_sent(0, 0)

        @pl.when(i == 2 * R + 1)
        def _():
            ag_fwd(1, 0)
            rs_half_load(0, 1)
            rs_half(0, 1)

        attend(lax.div(i, R), lax.rem(i, R))
        return carry

    lax.fori_loop(0, LEAD * R, lead, 0)
    ag_far(1, 0)
    rs_pair(0, 2)
    ag_fin(1, 0)
    h2_load(0).start()

    def gu_tile(j):
        slot = lax.rem(j, GU_SLOTS)

        @pl.when(j + GU_SLOTS - 1 < n_gu)
        def _():
            for cp in gu_copies(j + GU_SLOTS - 1, lax.rem(j + GU_SLOTS - 1, GU_SLOTS)):
                cp.start()

        for cp in gu_copies(j, slot):
            cp.wait()
        both = jnp.dot(h2v[...].reshape(n_dev * blk, width), gu_buf[slot], preferred_element_type=F32)
        gate, up = both[:, :GU], both[:, GU:]
        act[:, pl.ds(pl.multiple_of(j * GU, GU), GU)] = (jax.nn.silu(gate) * up).astype(BF)

    def dn_tile(j):
        slot = lax.rem(j, DN_SLOTS)

        @pl.when(j + 1 < n_dn)
        def _():
            dn_copy(j + 1, 1 - slot).start()

        dn_copy(j, slot).wait()
        tile = jnp.dot(act[...], dn_buf[slot], preferred_element_type=F32).astype(BF)
        pp[1, :, :, :, pl.ds(pl.multiple_of(j * DN, DN), DN)] = tile.reshape(n_chip, 2, blk, DN)

    def tiles(fn, part_idx, per):
        def one(i, carry):
            fn(part_idx * per + i)
            return carry

        lax.fori_loop(0, per, one, 0)

    last = n_chunks - 1
    done = (n_dn // DN_PARTS) * 3 * DN
    cuts = ((0, done, 0), (done, width - done, 1))

    def step(s, carry):
        nxt, att, old = s + 1, s + LEAD - 1, s - 1
        more = nxt < n_chunks
        has_att = (s > 0) & (att < n_chunks)

        def gu_part(k, carry):
            def at(when, cond, name, fn, chunk):
                @pl.when((k == when) & cond)
                def _():
                    fn(chunk)

            early = s == 0
            at(2, s > 0, "rs2_half", lambda c: rs_half(1, c), old)
            at(jnp.where(early, 1, 3), more, "rs1_relay", lambda c: rs_relay(0, c), nxt)
            at(5, s > 0, "rs2_relay", lambda c: rs_relay(1, c), old)
            at(jnp.where(early, 6, 8), more, "rs1_fin", rs1_fin, nxt)
            at(1, s > 0, "rs2_half_load", lambda c: rs_half_load(1, c), old)
            at(1, has_att, "ag1_fwd", lambda c: ag_fwd(0, c), att)
            at(jnp.where(early, 0, 2), more, "rs1_relay_load", lambda c: rs_relay_load(0, c), nxt)
            at(4, s > 0, "rs2_relay_load", lambda c: rs_relay_load(1, c), old)
            at(6, has_att, "ag1_far", lambda c: ag_far(0, c), att)
            at(7, has_att, "ready", ready, att)
            at(jnp.where(early, 5, 7), more, "rs1_fin_load", rs1_fin_load, nxt)

            @pl.when((k == GU_PARTS - 1) & has_att)
            def _():
                for cp in qa_loads():
                    cp.start()

            tiles(gu_tile, k, n_gu // GU_PARTS)
            return carry

        dn_copy(0, 0).start()
        h2_load(s).wait()
        lax.fori_loop(0, GU_PARTS, gu_part, 0)

        @pl.when(has_att)
        def _():
            for cp in qb_loads():
                cp.start()

        @pl.when(more & jnp.logical_not(has_att))
        def _():
            start_gu()

        @pl.when(more)
        def _():
            rs_sent(0, nxt)

        def att_step(r, carry):
            @pl.when((r == R - 1) & (s > 0))
            def _():
                rs2_fin_load(old)

            @pl.when(has_att)
            def _():
                attend(att, r)

            return carry

        lax.fori_loop(0, R, att_step, 0)

        @pl.when(has_att)
        def _():
            rs_pair(0, att)

        @pl.when(s > 0)
        def _():
            rs2_fin(old)

        def dn_part(k, carry):
            def at(when, cond, name, fn, chunk):
                @pl.when((k == when) & cond)
                def _():
                    fn(chunk)

            soon = has_att | (s == 0)

            def gathered(c):
                ag_fin(1, c)
                h2_load(c).start()

            at(2, att < n_chunks, "rs1_half", lambda c: rs_half(0, c), att)
            at(1, att < n_chunks, "rs1_half_load", lambda c: rs_half_load(0, c), att)
            at(jnp.where(soon, 0, 3), more, "ag2_fwd", lambda c: ag_fwd(1, c), nxt)
            at(0, att + 1 < n_chunks, "ag1_own", ag1_own, att + 1)
            at(jnp.where(has_att, 3, 2), more & soon, "ag2_far", lambda c: ag_far(1, c), nxt)
            at(4, more & soon, "ag2_fin", gathered, nxt)
            at(3, s == last, "tail_pair", lambda c: rs_pair(1, c, cuts[0]), s)
            at(4, s == last, "tail_half_load", lambda c: rs_half_load(1, c, cuts[0]), s)
            at(4, s == last, "tail_half", lambda c: rs_half(1, c, cuts[0]), s)
            tiles(dn_tile, k, n_dn // DN_PARTS)
            return carry

        lax.fori_loop(0, DN_PARTS, dn_part, 0)

        @pl.when(more & jnp.logical_not(has_att | (s == 0)))
        def _():
            ag_far(1, nxt)
            ag_fin(1, nxt)
            h2_load(nxt).start()

        @pl.when(more)
        def _():
            rs_pair(1, s)

        return carry

    lax.fori_loop(0, n_chunks, step, 0)

    rs_pair(1, last, cuts[1])
    x1_store(last).wait()
    out_store(last - 1).wait()
    xend_copy(last).start()
    rs_half_load(1, last, cuts[1])
    rs_half(1, last, cuts[1])
    for cut in cuts:
        rs_relay_load(1, last, cut)
        rs_relay(1, last, cut)
    xend_copy(last).wait()
    for cut in cuts:
        rs_fin_load(1, last, cut)
        rs2_add(last, cut)
    out_store(last).start()
    for cut in cuts:
        rs_sent(1, last, cut)
    out_store(last).wait()


def fused_layer(x, freq, bias, k_cache, v_cache, prefix, valid, g_attn, g_mlp, w_q, w_k, w_v, w_o, w_gate, w_up, w_down, n_dev):
    n_req, rows, width = x.shape
    n_chunks, blk = n_req // R, R * rows
    slots, hd = k_cache.shape[1:]
    tokens, qn, ffn = n_dev * rows, w_q.shape[1], w_gate.shape[1]
    n_chip = n_dev // 2
    hbm, smem, vmem = (pl.BlockSpec(memory_space=m) for m in (pl.ANY, pltpu.SMEM, pltpu.VMEM))
    chunked = lambda *s: jax.ShapeDtypeStruct((n_chunks, *s, width), BF)
    out_shape = [
        chunked(blk),
        jax.ShapeDtypeStruct(k_cache.shape, BF),
        jax.ShapeDtypeStruct(v_cache.shape, BF),
        chunked(n_dev, blk),
        chunked(n_dev, blk),
        chunked(n_chip, blk),
        chunked(n_chip, blk),
        chunked(2, rows),
        chunked(2, rows),
        chunked(2, blk),
        chunked(2, blk),
        chunked(blk),
        jax.ShapeDtypeStruct((n_req, tokens, hd), F32),
    ]
    dma = lambda *s: pltpu.SemaphoreType.DMA(s)
    rows_buf = pltpu.VMEM((blk, width), BF)
    scratch = [
        pltpu.VMEM((qn, width), BF),
        pltpu.VMEM((GU_SLOTS, width, 2 * GU), BF),
        pltpu.VMEM((DN_SLOTS, ffn, DN), BF),
        pltpu.VMEM((n_dev, blk, width), BF),
        pltpu.VMEM((n_dev, rows, width), BF),
        pltpu.VMEM((n_dev * blk, ffn), BF),
        pltpu.VMEM((2, n_chip, 2, blk, width), BF),
        *[rows_buf] * 6,
        pltpu.VMEM((2, blk, width), BF),
        pltpu.VMEM((1, blk, width), BF),
        *[pltpu.VMEM((slots, hd), BF)] * 2,
        pltpu.VMEM((2 * slots, hd), F32),
        pltpu.VMEM((tokens, hd), F32),
        pltpu.VMEM((2, tokens, slots), F32),
        dma(2, n_chunks, 9),
        dma(2, n_chunks, 9),
        dma(2, n_chunks + 1, 8),
        dma(2, n_chunks + 1, 8),
        dma(4),
        dma(3),
        dma(2, 2),
        dma(2),
        dma(4),
        dma(2),
        dma(GU_SLOTS, 2),
        dma(DN_SLOTS),
        dma(5),
        pltpu.SemaphoreType.DMA,
    ]
    res = pl.pallas_call(
        layer_kernel,
        in_specs=[smem, smem, vmem, vmem, vmem, vmem] + [hbm] * 10,
        out_specs=[hbm] * len(out_shape),
        out_shape=out_shape,
        scratch_shapes=scratch,
        compiler_params=pltpu.CompilerParams(vmem_limit_bytes=67_000_000, collective_id=0, has_side_effects=True),
        name="layer",
    )(prefix, valid, bias, g_attn[None], g_mlp[None], freq, x.reshape(n_chunks, blk, width), k_cache, v_cache, w_q, w_k, w_v, w_o, w_gate, w_up, w_down)
    return res[0].reshape(x.shape), res[1], res[2]


def solution(mesh):
    row_spec = P("dp", "tp", None)
    cache_spec = P("dp", None, "tp", None)
    req_spec = P("dp")
    rep_spec = P(None)
    col_spec = P(None, "tp")
    bias_spec = P("tp")
    down_spec = P("tp", None)
    n_dev = mesh.shape["tp"]

    def layer(x_rows, k_cache, v_cache, prefix, valid, g_attn, w_q, b_q, w_k, b_k, w_v, b_v, w_o, g_mlp, w_gate, w_up, w_down):
        n_req, rows, _ = x_rows.shape
        slots, hd = k_cache.shape[1], k_cache.shape[3]
        keys, vals = k_cache.reshape(n_req, slots, hd), v_cache.reshape(n_req, slots, hd)
        inv_freq = ROPE_THETA ** (-np.arange(0, hd, 2) / hd)
        freq = jnp.asarray(np.tile(inv_freq, 2)[None], F32)
        bias = jnp.concatenate([b_q, b_k, b_v])[None]
        out, k_out, v_out = fused_layer(x_rows, freq, bias, keys, vals, prefix, valid, g_attn, g_mlp, w_q, w_k, w_v, w_o, w_gate, w_up, w_down, n_dev)
        return out, k_out.reshape(k_cache.shape), v_out.reshape(v_cache.shape)

    in_specs = (row_spec, cache_spec, cache_spec, req_spec, req_spec, rep_spec, col_spec, bias_spec, col_spec, bias_spec, col_spec, bias_spec, down_spec, rep_spec, col_spec, col_spec, down_spec)
    return jax.shard_map(layer, mesh=mesh, in_specs=in_specs, out_specs=(row_spec, cache_spec, cache_spec), check_vma=False)
```

time: 826 us -> 639 us (0.77)
  Pallas kernels: 796 us -> 624 us
  other arithmetic: 9.65 us -> 0.72 us
    pallas_call x1, Pallas kernels: 796 us -> 624 us  [fused_layer(): pl.pallas_call(layer_kernel, in_specs=[smem, smem, vmem, vmem, vmem, vmem...]
where the time goes in v2:
time: 639 us; the launch traced here: 638 us
  Pallas kernels  624 us (98%)
  local copies, waits for them, and re-layouts  12.4 us (2%)
    pallas_call x1, Pallas kernels, fused_layer(): pl.pallas_call(layer_kernel, in_specs=[smem, smem, vmem, vmem, vmem, vmem...  624 us

profile of v2, /device:TPU:112, one launch (start us, length us, event | category | flops | bytes accessed | tf_op | source)
XLA Modules:
  0.0 637.7 jit_solution(17184540603556594019)
XLA Ops:
  0.6 0.7 pad_maximum_fusion
  1.4 0.6 broadcast_in_dim.9.bias_ref
  1.9 1.3 broadcast_in_dim.10.g1_ref
  3.3 1.3 broadcast_in_dim.11.g2_ref
  4.6 624.0 %layer.1 = (bf16[6,64,5120]{2,1,0:T(8,128)(2,1)}, bf16[12,1024,128]{2,1,0:T(8,128)(2,1)}, bf16[12,1024,128]{2,1,0:T(8,128)(2,1)}, bf16[6,8,64,5120]{3,2,1,0:T(8,...) custom-call(s32[12]{0:T(128)} %p_ref.1, s32[12]{0:T(128)} %c_ref.1, ...), custom_call_target="tpu_custom_call" | custom-call | tf_op jit(solution)/shard_map/layer/pallas_call | solution.py:702
  628.6 0.0 copy-start.1
  628.6 4.4 copy.26
  633.0 0.0 copy-done.1
  633.0 0.0 copy-start
  633.0 1.7 copy.27
  634.7 1.4 copy-done
  636.1 1.7 copy.28
Async XLA Ops:
  628.6 4.5 copy-start.1
  633.0 3.0 copy-start

commit v3 on v2

--- a/solution.py
+++ b/solution.py
@@ -1,3 +1,5 @@
+import functools
+
 import jax
 import jax.numpy as jnp
 import numpy as np
@@ -16,6 +18,7 @@
 DN = 512
 GU_SLOTS, DN_SLOTS = 2, 2
 QA = 512
+ATT, MLP = 0, 1
 SUB = 16
 LEAD = 3
 
@@ -23,7 +26,7 @@
 
 
 def layer_kernel(
-    p_ref, c_ref, bias_ref, g1_ref, g2_ref, freq_ref, x_hbm, kc_hbm, vc_hbm, wq_hbm, wk_hbm, wv_hbm, wo_hbm, wg_hbm, wu_hbm, wd_hbm,
+    p_ref, c_ref, bq_ref, bk_ref, bv_ref, g1_ref, g2_ref, freq_ref, x_hbm, kc_hbm, vc_hbm, wq_hbm, wk_hbm, wv_hbm, wo_hbm, wg_hbm, wu_hbm, wd_hbm,
     out_hbm, ko_hbm, vo_hbm, h1_hbm, h2_hbm, sb1_hbm, sb2_hbm, rb1_hbm, rb2_hbm, fb1_hbm, fb2_hbm, x1_hbm, cs_hbm,
     w_out, gu_buf, dn_buf, h2v, h1v, act, pp, t_a, t_b, t_c, xin, xmid, xend, hb1, hb2, kb, vb, shift, csv, sbuf,
     ag_s, ag_r, rs_s, rs_r, tmp_sem, x_sem, h_sem, st_sem, at_sem, kv_sem, gu_sem, dn_sem, w_sem, h2_sem,
@@ -49,8 +52,11 @@
     h_all = (h1_hbm, h2_hbm)
     sbs, rbs, fbs = (sb1_hbm, sb2_hbm), (rb1_hbm, rb2_hbm), (fb1_hbm, fb2_hbm)
 
+    def p_slot(s, c):
+        return jnp.where(c == n_chunks - 2, 0, 1) if s else jnp.where(c == 1, 1, 0)
+
     def part(s, c):
-        return pp.at[1 if s else jnp.where(c == 1, 1, 0)]
+        return pp.at[p_slot(s, c)]
 
     def h_slot(s, c):
         return 0 if s else lax.rem(c, 2)
@@ -61,8 +67,10 @@
         lt, rt, ft = 2 * left_chip + core, 2 * right_chip + core, 2 * far + core
         own = hbufs[s].at[h_slot(s, c)]
         src, dst, dev = [
-            (own, h.at[c, me], right),
-            (own, h.at[c, me], left),
+            (own.at[lo], h.at[c, me, lo], right),
+            (own.at[hi], h.at[c, me, hi], right),
+            (own.at[hi], h.at[c, me, hi], left),
+            (own.at[lo], h.at[c, me, lo], left),
             (own, h.at[c, me], sib),
             (h.at[c, lt, lo], h.at[c, lt, lo], right),
             (h.at[c, rt, hi], h.at[c, rt, hi], left),
@@ -71,10 +79,11 @@
             (h.at[c, ft, lo], h.at[c, ft, lo], sib),
             (h.at[c, ft, hi], h.at[c, ft, hi], sib),
         ][k]
-        return pltpu.make_async_remote_copy(src, dst, ag_s.at[s, c, k], ag_r.at[s, c, k], device_id={"tp": dev})
+        return pltpu.make_async_remote_copy(src, dst, ag_s.at[s, lax.rem(c, 2), k], ag_r.at[s, c, k], device_id={"tp": dev})
 
     def rs(s, c, k, cut=None):
-        col, row = (pl.ds(0, width), c) if cut is None else (pl.ds(*cut[:2]), n_chunks - 1 + cut[2])
+        col, got = (pl.ds(0, width), c) if cut is None else (pl.ds(*cut[:2]), n_chunks - 1 + cut[2])
+        sent = (s, lax.rem(c, 2)) if cut is None or cut[2] == 0 else (0, cut[2] - 1)
         p, lo, hi = part(s, c), pl.ds(0, half), pl.ds(half, half)
         all_rows = pl.ds(0, blk)
         if k < 4:
@@ -83,10 +92,12 @@
             src, dst, dev = [
                 (p.at[far, core, lo, col], rbs[s].at[c, 0, pl.ds(0, half), col], right),
                 (p.at[far, core, hi, col], rbs[s].at[c, 1, pl.ds(0, half), col], left),
-                (p.at[right_chip, core, all_rows, col], fbs[s].at[c, 0, all_rows, col], right),
-                (p.at[left_chip, core, all_rows, col], fbs[s].at[c, 1, all_rows, col], left),
+                (p.at[right_chip, core, hi, col], fbs[s].at[c, 0, hi, col], right),
+                (p.at[left_chip, core, lo, col], fbs[s].at[c, 1, lo, col], left),
+                (p.at[right_chip, core, lo, col], fbs[s].at[c, 0, lo, col], right),
+                (p.at[left_chip, core, hi, col], fbs[s].at[c, 1, hi, col], left),
             ][k - 4]
-        return pltpu.make_async_remote_copy(src, dst, rs_s.at[s, row, k], rs_r.at[s, row, k], device_id={"tp": dev})
+        return pltpu.make_async_remote_copy(src, dst, rs_s.at[*sent, k], rs_r.at[s, got, k], device_id={"tp": dev})
 
     def by_rows(rows, fn):
         def step(i, carry):
@@ -98,9 +109,12 @@
     def f32(v):
         return v.astype(F32)
 
+    def row(v):
+        return f32(v).reshape(1, v.shape[0])
+
     def normed(wide, gain):
         inv_rms = lax.rsqrt(jnp.mean(wide * wide, axis=-1, keepdims=True) + NORM_EPS)
-        return (wide * inv_rms * f32(gain[...])).astype(BF)
+        return (wide * inv_rms * row(gain[...])).astype(BF)
 
     def own_copy(s, c):
         slot = h_slot(s, c)
@@ -111,17 +125,17 @@
 
     def ag_send(s, c):
         own_copy(s, c).start()
-        for k in range(3):
+        for k in (0, 2, 1, 3, 4):
             ag(s, c, k).start()
 
     def ag1_own(c):
         x_copy(c).wait()
 
         def fn(rows):
-            hb1[h_slot(0, c), rows, :] = normed(f32(xin[rows, :]), g1_ref)
+            hb1[h_slot(ATT, c), rows, :] = normed(f32(xin[rows, :]), g1_ref)
 
         by_rows(blk, fn)
-        ag_send(0, c)
+        ag_send(ATT, c)
 
         @pl.when(c + 1 < n_chunks)
         def _():
@@ -129,21 +143,19 @@
 
     def ag_fwd(s, c):
         ag(s, c, 0).wait_recv()
-        ag(s, c, 3).start()
-        ag(s, c, 1).wait_recv()
-        ag(s, c, 4).start()
         ag(s, c, 5).start()
+        ag(s, c, 2).wait_recv()
         ag(s, c, 6).start()
 
     def ag_far(s, c):
-        for k in (3, 4):
+        for got, send in ((1, 7), (3, 8), (5, 9), (6, 10)):
+            ag(s, c, got).wait_recv()
+            ag(s, c, send).start()
+
+    def ag_fin(s, c):
+        for k in (4, 7, 8, 9, 10):
             ag(s, c, k).wait_recv()
-            ag(s, c, k + 4).start()
-
-    def ag_fin(s, c):
-        for k in (2, 5, 6, 7, 8):
-            ag(s, c, k).wait_recv()
-        for k in range(9):
+        for k in range(11):
             ag(s, c, k).wait_send()
         own_copy(s, c).wait()
 
@@ -152,64 +164,74 @@
             rs(s, c, k, cut).start()
 
     def loads(srcs, cut):
-        col = pl.ds(0, width) if cut is None else pl.ds(*cut[:2])
-        return [
-            pltpu.make_async_copy(src.at[:, col], dst.at[:, col], tmp_sem.at[i]) for i, (src, dst) in enumerate(srcs)
-        ]
+        col, row_idx = (pl.ds(0, width), 0) if cut is None else (pl.ds(*cut[:2]), cut[2])
+        return [pltpu.make_async_copy(src.at[:, col], dst.at[:, col], tmp_sem.at[row_idx, i]) for i, (src, dst) in enumerate(srcs)]
+
+    lo_rows, hi_rows = pl.ds(0, half), pl.ds(half, half)
 
     def half_loads(s, c, cut):
-        return loads([(sbs[s].at[c, 0], t_a)], cut)
+        sb = sbs[s]
+        return loads([(sb.at[c, 0], t_a), (sb.at[c, 1, hi_rows], t_b.at[hi_rows]), (sb.at[c, 2, lo_rows], t_b.at[lo_rows])], cut)
 
     def rs_half_load(s, c, cut=None):
-        rs(s, c, 0, cut).wait_recv()
-        for cp in half_loads(s, c, cut):
+        for k, cp in enumerate(half_loads(s, c, cut)):
+            rs(s, c, k, cut).wait_recv()
             cp.start()
 
-    def rs_half(s, c, cut=None):
+    def halves(fn):
+        def step(i, carry):
+            fn(pl.ds(pl.multiple_of(i * SUB, SUB), SUB), pl.ds(pl.multiple_of(half + i * SUB, SUB), SUB))
+            return carry
+
+        lax.fori_loop(0, half // SUB, step, 0)
+
+    def rs_half(s, c, cut=None, eager=False):
         for cp in half_loads(s, c, cut):
             cp.wait()
         p, col = part(s, c), slice(None) if cut is None else pl.ds(*cut[:2])
 
-        def fn(rows):
-            p[far, core, rows, col] = (f32(p[far, core, rows, col]) + f32(t_a[rows, col])).astype(BF)
-
-        by_rows(blk, fn)
-        rs(s, c, 4, cut).start()
-        rs(s, c, 5, cut).start()
+        def fn(lo, hi):
+            for rows in (lo, hi):
+                p[far, core, rows, col] = (f32(p[far, core, rows, col]) + f32(t_a[rows, col])).astype(BF)
+            p[right_chip, core, hi, col] = (f32(p[right_chip, core, hi, col]) + f32(t_b[hi, col])).astype(BF)
+            p[left_chip, core, lo, col] = (f32(p[left_chip, core, lo, col]) + f32(t_b[lo, col])).astype(BF)
+
+        halves(fn)
+        for k in range(4, 8 if eager else 6):
+            rs(s, c, k, cut).start()
 
     def relay_loads(s, c, cut):
-        lo, hi = t_c.at[pl.ds(0, half)], t_c.at[pl.ds(half, half)]
-        return loads([(sbs[s].at[c, 1], t_a), (sbs[s].at[c, 2], t_b), (rbs[s].at[c, 0], lo), (rbs[s].at[c, 1], hi)], cut)
+        sb, rb = sbs[s], rbs[s]
+        return loads(
+            [(sb.at[c, 1, lo_rows], t_a.at[lo_rows]), (sb.at[c, 2, hi_rows], t_a.at[hi_rows]), (rb.at[c, 0], t_c.at[lo_rows]), (rb.at[c, 1], t_c.at[hi_rows])], cut
+        )
 
     def rs_relay_load(s, c, cut=None):
-        for k, cp in zip((1, 2, 4, 5), relay_loads(s, c, cut)):
+        for k in (4, 5):
             rs(s, c, k, cut).wait_recv()
+        for cp in relay_loads(s, c, cut):
             cp.start()
 
-    def rs_relay(s, c, cut=None):
+    def rs_relay(s, c, cut=None, eager=False):
         for cp in relay_loads(s, c, cut):
             cp.wait()
         p, col = part(s, c), slice(None) if cut is None else pl.ds(*cut[:2])
 
-        def step(i, carry):
-            lo = pl.ds(pl.multiple_of(i * SUB, SUB), SUB)
-            hi = pl.ds(pl.multiple_of(half + i * SUB, SUB), SUB)
+        def fn(lo, hi):
             p[right_chip, core, lo, col] = (f32(p[right_chip, core, lo, col]) + f32(t_a[lo, col]) + f32(t_c[lo, col])).astype(BF)
-            p[right_chip, core, hi, col] = (f32(p[right_chip, core, hi, col]) + f32(t_a[hi, col])).astype(BF)
-            p[left_chip, core, lo, col] = (f32(p[left_chip, core, lo, col]) + f32(t_b[lo, col])).astype(BF)
-            p[left_chip, core, hi, col] = (f32(p[left_chip, core, hi, col]) + f32(t_b[hi, col]) + f32(t_c[hi, col])).astype(BF)
-            return carry
-
-        lax.fori_loop(0, half // SUB, step, 0)
-        rs(s, c, 6, cut).start()
-        rs(s, c, 7, cut).start()
+            p[left_chip, core, hi, col] = (f32(p[left_chip, core, hi, col]) + f32(t_a[hi, col]) + f32(t_c[hi, col])).astype(BF)
+
+        halves(fn)
+        for k in (8, 9) if eager else (8, 9, 6, 7):
+            rs(s, c, k, cut).start()
 
     def fin_loads(s, c, cut):
         return loads([(sbs[s].at[c, 3], t_a), (fbs[s].at[c, 0], t_b), (fbs[s].at[c, 1], t_c)], cut)
 
     def rs_fin_load(s, c, cut=None):
-        for k, cp in zip((3, 6, 7), fin_loads(s, c, cut)):
+        for k in (3, 6, 7, 8, 9):
             rs(s, c, k, cut).wait_recv()
+        for cp in fin_loads(s, c, cut):
             cp.start()
 
     def rs_total(s, c, rows, col=slice(None)):
@@ -217,7 +239,7 @@
         return (f32(p[chip, core, rows, col]) + f32(t_a[rows, col]) + f32(t_b[rows, col]) + f32(t_c[rows, col])).astype(BF)
 
     def rs_sent(s, c, cut=None):
-        for k in range(8):
+        for k in range(10):
             rs(s, c, k, cut).wait_send()
 
     def xmid_copy(c):
@@ -238,21 +260,21 @@
             x1_store(c - 1).wait()
 
         xmid_copy(c).start()
-        rs_fin_load(0, c)
+        rs_fin_load(ATT, c)
 
     def rs1_fin(c):
-        for cp in fin_loads(0, c, None):
+        for cp in fin_loads(ATT, c, None):
             cp.wait()
         xmid_copy(c).wait()
 
         def fn(rows):
-            mid = (f32(xmid[rows, :]) + f32(rs_total(0, c, rows))).astype(BF)
+            mid = (f32(xmid[rows, :]) + f32(rs_total(ATT, c, rows))).astype(BF)
             xmid[rows, :] = mid
             hb2[0, rows, :] = normed(f32(mid), g2_ref)
 
         by_rows(blk, fn)
         x1_store(c).start()
-        ag_send(1, c)
+        ag_send(MLP, c)
 
     def rs2_fin_load(c):
         @pl.when(c > 0)
@@ -260,15 +282,15 @@
             out_store(c - 1).wait()
 
         xend_copy(c).start()
-        rs_fin_load(1, c)
+        rs_fin_load(MLP, c)
 
     def rs2_add(c, cut=None):
-        for cp in fin_loads(1, c, cut):
+        for cp in fin_loads(MLP, c, cut):
             cp.wait()
         col = slice(None) if cut is None else pl.ds(*cut[:2])
 
         def fn(rows):
-            xend[rows, col] = (f32(xend[rows, col]) + f32(rs_total(1, c, rows, col))).astype(BF)
+            xend[rows, col] = (f32(xend[rows, col]) + f32(rs_total(MLP, c, rows, col))).astype(BF)
 
         by_rows(blk, fn)
 
@@ -276,7 +298,7 @@
         xend_copy(c).wait()
         rs2_add(c)
         out_store(c).start()
-        rs_sent(1, c)
+        rs_sent(MLP, c)
 
     def att_loads(a, r):
         return (
@@ -302,23 +324,23 @@
 
     def attend(a, r):
         req = a * R + r
-        p_out = part(0, a)
+        p_out = part(ATT, a)
         for cp in (*att_loads(a, r), *cache_loads(a, r)):
             cp.wait()
         fresh = (r == 0) & ((a == 0) | (a >= LEAD))
         h = h1v[...].reshape(tokens, width)
 
-        def project(cps, slot, lo, size):
+        def project(cps, slot, bias):
             @pl.when(fresh)
             def _():
                 for cp in cps:
                     cp.wait()
 
-            total = jnp.dot(h, gu_buf[slot, :, 0:size], preferred_element_type=F32)
-            return f32((total + f32(bias_ref[:, lo : lo + size])).astype(BF))
-
-        some_q = project(qa_loads(), 1, 0, QA)
-        rest = project(qb_loads(), 0, QA, qn + 2 * hd - QA)
+            total = jnp.dot(h, gu_buf[slot, :, 0 : bias.shape[1]], preferred_element_type=F32)
+            return f32((total + bias).astype(BF))
+
+        some_q = project(qa_loads(), 1, row(bq_ref[0:QA]))
+        rest = project(qb_loads(), 0, jnp.concatenate([row(bq_ref[QA:qn]), row(bk_ref[...]), row(bv_ref[...])], axis=1))
         p, c = p_ref[req], c_ref[req]
         cs = csv[...]
         sc = pltpu.roll(cs, hd // 2, 1)
@@ -420,64 +442,69 @@
     for cp in (*qa_loads(), *qb_loads(), wo_copy):
         cp.start()
     shift[...] = jnp.zeros_like(shift)
-    lax.fori_loop(0, n_chunks * R, table, 0)
+    lax.fori_loop(0, 2 * n_chunks * R // 3, table, 0)
+    ag_fwd(ATT, 0)
+    lax.fori_loop(2 * n_chunks * R // 3, n_chunks * R, table, 0)
     wo_copy.wait()
 
     def ready(c):
-        ag_fin(0, c)
+        ag_fin(ATT, c)
         for cp in (*att_loads(c, 0), *cache_loads(c, 0)):
             cp.start()
 
     def lead(i, carry):
         @pl.when(i == 0)
         def _():
-            ag_fwd(0, 0)
             ag1_own(1)
-            ag_far(0, 0)
+            ag_far(ATT, 0)
             ready(0)
 
         @pl.when(i == 1)
         def _():
-            ag_fwd(0, 1)
+            ag_fwd(ATT, 1)
             ag1_own(2)
 
         @pl.when(i == R)
         def _():
-            ag_far(0, 1)
-            rs_pair(0, 0)
+            ag_far(ATT, 1)
+            rs_pair(ATT, 0)
             ready(1)
-            rs_half_load(0, 0)
-            rs_half(0, 0)
+            rs_half_load(ATT, 0)
+            rs_half(ATT, 0, eager=True)
 
         @pl.when(i == R + 1)
         def _():
-            ag_fwd(0, 2)
-            rs_relay_load(0, 0)
-            rs_relay(0, 0)
+            rs_relay_load(ATT, 0)
+            rs_relay(ATT, 0, eager=True)
+            ag_fwd(ATT, 2)
 
         @pl.when(i == 2 * R)
         def _():
-            ag_far(0, 2)
-            rs_pair(0, 1)
+            rs_pair(ATT, 1)
             rs1_fin_load(0)
             rs1_fin(0)
+            ag_far(ATT, 2)
             ready(2)
-            rs_sent(0, 0)
+            rs_sent(ATT, 0)
 
         @pl.when(i == 2 * R + 1)
         def _():
-            ag_fwd(1, 0)
-            rs_half_load(0, 1)
-            rs_half(0, 1)
+            ag_fwd(MLP, 0)
+            rs_half_load(ATT, 1)
+            rs_half(ATT, 1)
 
         attend(lax.div(i, R), lax.rem(i, R))
         return carry
 
     lax.fori_loop(0, LEAD * R, lead, 0)
-    ag_far(1, 0)
-    rs_pair(0, 2)
-    ag_fin(1, 0)
+    ag_far(MLP, 0)
+    rs_pair(ATT, 2)
+    ag_fin(MLP, 0)
     h2_load(0).start()
+
+    last = n_chunks - 1
+    unit = (n_dn // DN_PARTS) * DN
+    cuts = ((0, 2 * unit, 0), (2 * unit, 2 * unit, 1), (4 * unit, width - 4 * unit, 2))
 
     def gu_tile(j):
         slot = lax.rem(j, GU_SLOTS)
@@ -493,8 +520,15 @@
         gate, up = both[:, :GU], both[:, GU:]
         act[:, pl.ds(pl.multiple_of(j * GU, GU), GU)] = (jax.nn.silu(gate) * up).astype(BF)
 
-    def dn_tile(j):
+    def dn_tile(s, j):
         slot = lax.rem(j, DN_SLOTS)
+
+        @pl.when((s == last) & (j == n_dn - 1))
+        def _():
+            rs_relay_load(MLP, last, cuts[0])
+            rs_half_load(MLP, last, cuts[1])
+            rs_relay(MLP, last, cuts[0], True)
+            rs_half(MLP, last, cuts[1], True)
 
         @pl.when(j + 1 < n_dn)
         def _():
@@ -502,7 +536,7 @@
 
         dn_copy(j, slot).wait()
         tile = jnp.dot(act[...], dn_buf[slot], preferred_element_type=F32).astype(BF)
-        pp[1, :, :, :, pl.ds(pl.multiple_of(j * DN, DN), DN)] = tile.reshape(n_chip, 2, blk, DN)
+        pp[p_slot(MLP, s), :, :, :, pl.ds(pl.multiple_of(j * DN, DN), DN)] = tile.reshape(n_chip, 2, blk, DN)
 
     def tiles(fn, part_idx, per):
         def one(i, carry):
@@ -510,10 +544,6 @@
             return carry
 
         lax.fori_loop(0, per, one, 0)
-
-    last = n_chunks - 1
-    done = (n_dn // DN_PARTS) * 3 * DN
-    cuts = ((0, done, 0), (done, width - done, 1))
 
     def step(s, carry):
         nxt, att, old = s + 1, s + LEAD - 1, s - 1
@@ -526,18 +556,21 @@
                 def _():
                     fn(chunk)
 
-            early = s == 0
-            at(2, s > 0, "rs2_half", lambda c: rs_half(1, c), old)
-            at(jnp.where(early, 1, 3), more, "rs1_relay", lambda c: rs_relay(0, c), nxt)
-            at(5, s > 0, "rs2_relay", lambda c: rs_relay(1, c), old)
-            at(jnp.where(early, 6, 8), more, "rs1_fin", rs1_fin, nxt)
-            at(1, s > 0, "rs2_half_load", lambda c: rs_half_load(1, c), old)
-            at(1, has_att, "ag1_fwd", lambda c: ag_fwd(0, c), att)
-            at(jnp.where(early, 0, 2), more, "rs1_relay_load", lambda c: rs_relay_load(0, c), nxt)
-            at(4, s > 0, "rs2_relay_load", lambda c: rs_relay_load(1, c), old)
-            at(6, has_att, "ag1_far", lambda c: ag_far(0, c), att)
+            early, pen = s == 0, s == last - 1
+            pick = lambda att_at, pen_at, else_at: jnp.where(has_att, att_at, jnp.where(pen, pen_at, else_at))
+            at(0, pen, "rs1_relay", lambda c: rs_relay(ATT, c), nxt)
+            at(2, s > 0, "rs2_half", lambda c: rs_half(MLP, c), old)
+            at(jnp.where(early, 1, 3), s < last - 1, "rs1_relay", lambda c: rs_relay(ATT, c), nxt)
+            at(8, pen, "ag2_fwd", lambda c: ag_fwd(MLP, c), nxt)
+            at(pick(6, 8, 5), s > 0, "rs2_relay", lambda c: rs_relay(MLP, c), old)
+            at(pick(-1, 5, 6), more, "rs1_fin", rs1_fin, nxt)
+            at(1, s > 0, "rs2_half_load", lambda c: rs_half_load(MLP, c), old)
+            at(1, has_att, "ag1_fwd", lambda c: ag_fwd(ATT, c), att)
+            at(jnp.where(early, 0, 2), s < last - 1, "rs1_relay_load", lambda c: rs_relay_load(ATT, c), nxt)
+            at(pick(5, 7, 4), s > 0, "rs2_relay_load", lambda c: rs_relay_load(MLP, c), old)
+            at(6, has_att, "ag1_far", lambda c: ag_far(ATT, c), att)
             at(7, has_att, "ready", ready, att)
-            at(jnp.where(early, 5, 7), more, "rs1_fin_load", rs1_fin_load, nxt)
+            at(pick(8, 4, 5), more, "rs1_fin_load", rs1_fin_load, nxt)
 
             @pl.when((k == GU_PARTS - 1) & has_att)
             def _():
@@ -555,6 +588,7 @@
         def _():
             for cp in qb_loads():
                 cp.start()
+            rs1_fin(nxt)
 
         @pl.when(more & jnp.logical_not(has_att))
         def _():
@@ -562,10 +596,10 @@
 
         @pl.when(more)
         def _():
-            rs_sent(0, nxt)
+            rs_sent(ATT, nxt)
 
         def att_step(r, carry):
-            @pl.when((r == R - 1) & (s > 0))
+            @pl.when((r == R - 1) & has_att)
             def _():
                 rs2_fin_load(old)
 
@@ -579,10 +613,7 @@
 
         @pl.when(has_att)
         def _():
-            rs_pair(0, att)
-
-        @pl.when(s > 0)
-        def _():
+            rs_pair(ATT, att)
             rs2_fin(old)
 
         def dn_part(k, carry):
@@ -591,60 +622,66 @@
                 def _():
                     fn(chunk)
 
-            soon = has_att | (s == 0)
+            pen = s == last - 1
+            pick = lambda att_at, pen_at, else_at: jnp.where(has_att, att_at, jnp.where(pen, pen_at, else_at))
 
             def gathered(c):
-                ag_fin(1, c)
-                h2_load(c).start()
-
-            at(2, att < n_chunks, "rs1_half", lambda c: rs_half(0, c), att)
-            at(1, att < n_chunks, "rs1_half_load", lambda c: rs_half_load(0, c), att)
-            at(jnp.where(soon, 0, 3), more, "ag2_fwd", lambda c: ag_fwd(1, c), nxt)
+                ag_fin(MLP, c)
+                h2_load(c).start(priority=1)
+
+            at(2, s == last, "rs2_fin", rs2_fin, old)
+            at(2, att < n_chunks, "rs1_half", lambda c: rs_half(ATT, c), att)
+            at(1, att < n_chunks, "rs1_half_load", lambda c: rs_half_load(ATT, c), att)
+            at(0, more & jnp.logical_not(pen), "ag2_fwd", lambda c: ag_fwd(MLP, c), nxt)
             at(0, att + 1 < n_chunks, "ag1_own", ag1_own, att + 1)
-            at(jnp.where(has_att, 3, 2), more & soon, "ag2_far", lambda c: ag_far(1, c), nxt)
-            at(4, more & soon, "ag2_fin", gathered, nxt)
-            at(3, s == last, "tail_pair", lambda c: rs_pair(1, c, cuts[0]), s)
-            at(4, s == last, "tail_half_load", lambda c: rs_half_load(1, c, cuts[0]), s)
-            at(4, s == last, "tail_half", lambda c: rs_half(1, c, cuts[0]), s)
-            tiles(dn_tile, k, n_dn // DN_PARTS)
+            at(pick(3, 1, 2), more, "ag2_far", lambda c: ag_far(MLP, c), nxt)
+            at(pick(4, 2, 4), more, "ag2_fin", gathered, nxt)
+            at(4, s == last - 2, "rs1_relay_load", lambda c: rs_relay_load(ATT, c), att)
+            at(jnp.where(pen, 4, 1), pen | (s == last), "rs2_fin_load", rs2_fin_load, old)
+            at(2, s == last, "tail_pair", lambda c: rs_pair(MLP, c, cuts[0]), s)
+            at(3, s == last, "tail_half_load", lambda c: rs_half_load(MLP, c, cuts[0]), s)
+            at(3, s == last, "tail_half", lambda c: rs_half(MLP, c, cuts[0], True), s)
+            at(4, s == last, "tail_pair", lambda c: rs_pair(MLP, c, cuts[1]), s)
+            tiles(functools.partial(dn_tile, s), k, n_dn // DN_PARTS)
             return carry
 
         lax.fori_loop(0, DN_PARTS, dn_part, 0)
 
-        @pl.when(more & jnp.logical_not(has_att | (s == 0)))
-        def _():
-            ag_far(1, nxt)
-            ag_fin(1, nxt)
-            h2_load(nxt).start()
+        @pl.when(s == last - 1)
+        def _():
+            rs2_fin(old)
 
         @pl.when(more)
         def _():
-            rs_pair(1, s)
+            rs_pair(MLP, s)
 
         return carry
 
     lax.fori_loop(0, n_chunks, step, 0)
 
-    rs_pair(1, last, cuts[1])
+    rs_pair(MLP, last, cuts[2])
+    rs_half_load(MLP, last, cuts[2])
+    rs_half(MLP, last, cuts[2], True)
     x1_store(last).wait()
     out_store(last - 1).wait()
     xend_copy(last).start()
-    rs_half_load(1, last, cuts[1])
-    rs_half(1, last, cuts[1])
-    for cut in cuts:
-        rs_relay_load(1, last, cut)
-        rs_relay(1, last, cut)
     xend_copy(last).wait()
-    for cut in cuts:
-        rs_fin_load(1, last, cut)
+    rs_fin_load(MLP, last, cuts[0])
+    rs_relay_load(MLP, last, cuts[1])
+    rs_relay(MLP, last, cuts[1], True)
+    rs2_add(last, cuts[0])
+    rs_relay_load(MLP, last, cuts[2])
+    rs_relay(MLP, last, cuts[2], True)
+    for cut in cuts[1:]:
+        rs_fin_load(MLP, last, cut)
         rs2_add(last, cut)
     out_store(last).start()
     for cut in cuts:
-        rs_sent(1, last, cut)
+        rs_sent(MLP, last, cut)
     out_store(last).wait()
 
 
-def fused_layer(x, freq, bias, k_cache, v_cache, prefix, valid, g_attn, g_mlp, w_q, w_k, w_v, w_o, w_gate, w_up, w_down, n_dev):
+def fused_layer(x, freq, b_q, b_k, b_v, k_cache, v_cache, prefix, valid, g_attn, g_mlp, w_q, w_k, w_v, w_o, w_gate, w_up, w_down, n_dev):
     n_req, rows, width = x.shape
     n_chunks, blk = n_req // R, R * rows
     slots, hd = k_cache.shape[1:]
@@ -684,11 +721,11 @@
         pltpu.VMEM((2 * slots, hd), F32),
         pltpu.VMEM((tokens, hd), F32),
         pltpu.VMEM((2, tokens, slots), F32),
-        dma(2, n_chunks, 9),
-        dma(2, n_chunks, 9),
-        dma(2, n_chunks + 1, 8),
-        dma(2, n_chunks + 1, 8),
-        dma(4),
+        dma(2, 2, 11),
+        dma(2, n_chunks, 11),
+        dma(2, 2, 10),
+        dma(2, n_chunks + 2, 10),
+        dma(3, 4),
         dma(3),
         dma(2, 2),
         dma(2),
@@ -701,13 +738,13 @@
     ]
     res = pl.pallas_call(
         layer_kernel,
-        in_specs=[smem, smem, vmem, vmem, vmem, vmem] + [hbm] * 10,
+        in_specs=[smem, smem] + [vmem] * 6 + [hbm] * 10,
         out_specs=[hbm] * len(out_shape),
         out_shape=out_shape,
         scratch_shapes=scratch,
         compiler_params=pltpu.CompilerParams(vmem_limit_bytes=67_000_000, collective_id=0, has_side_effects=True),
         name="layer",
-    )(prefix, valid, bias, g_attn[None], g_mlp[None], freq, x.reshape(n_chunks, blk, width), k_cache, v_cache, w_q, w_k, w_v, w_o, w_gate, w_up, w_down)
+    )(prefix, valid, b_q, b_k, b_v, g_attn, g_mlp, freq, x.reshape(n_chunks, blk, width), k_cache, v_cache, w_q, w_k, w_v, w_o, w_gate, w_up, w_down)
     return res[0].reshape(x.shape), res[1], res[2]
 
 
@@ -727,8 +764,7 @@
         keys, vals = k_cache.reshape(n_req, slots, hd), v_cache.reshape(n_req, slots, hd)
         inv_freq = ROPE_THETA ** (-np.arange(0, hd, 2) / hd)
         freq = jnp.asarray(np.tile(inv_freq, 2)[None], F32)
-        bias = jnp.concatenate([b_q, b_k, b_v])[None]
-        out, k_out, v_out = fused_layer(x_rows, freq, bias, keys, vals, prefix, valid, g_attn, g_mlp, w_q, w_k, w_v, w_o, w_gate, w_up, w_down, n_dev)
+        out, k_out, v_out = fused_layer(x_rows, freq, b_q, b_k, b_v, keys, vals, prefix, valid, g_attn, g_mlp, w_q, w_k, w_v, w_o, w_gate, w_up, w_down, n_dev)
         return out, k_out.reshape(k_cache.shape), v_out.reshape(v_cache.shape)
 
     in_specs = (row_spec, cache_spec, cache_spec, req_spec, req_spec, rep_spec, col_spec, bias_spec, col_spec, bias_spec, col_spec, bias_spec, down_spec, rep_spec, col_spec, col_spec, down_spec)

time: 639 us -> 604 us (0.945)
  Pallas kernels: 624 us -> 594 us
    pallas_call x1, Pallas kernels: 624 us -> 594 us  [fused_layer(): pl.pallas_call(layer_kernel, in_specs=[smem, smem] + [vmem] * 6 + [hbm] *...]
where the time goes in v3:
time: 604 us; the launch traced here: 603 us
  Pallas kernels  594 us (98%)
  local copies, waits for them, and re-layouts  9.13 us (2%)
    pallas_call x1, Pallas kernels, fused_layer(): pl.pallas_call(layer_kernel, in_specs=[smem, smem] + [vmem] * 6 + [hbm] *...  594 us

profile of v3, /device:TPU:112, one launch (start us, length us, event | category | flops | bytes accessed | tf_op | source)
XLA Modules:
  0.0 603.3 jit_solution(7794173804858980055)
XLA Ops:
  0.6 593.6 %layer.1 = (bf16[6,64,5120]{2,1,0:T(8,128)(2,1)}, bf16[12,1024,128]{2,1,0:T(8,128)(2,1)}, bf16[12,1024,128]{2,1,0:T(8,128)(2,1)}, bf16[6,8,64,5120]{3,2,1,0:T(8,...) custom-call(s32[12]{0:T(128)} %p_ref.1, s32[12]{0:T(128)} %c_ref.1, ...), custom_call_target="tpu_custom_call" | custom-call | tf_op jit(solution)/shard_map/layer/pallas_call | solution.py:739
  594.2 0.0 copy-start.1
  594.2 4.4 copy.26
  598.6 0.0 copy-done.1
  598.6 0.0 copy-start
  598.7 1.7 copy.27
  600.3 1.4 copy-done
  601.7 1.7 copy.28
Async XLA Ops:
  594.2 4.5 copy-start.1
  598.6 3.0 copy-start

commit v4 on v3

--- a/solution.py
+++ b/solution.py
@@ -679,6 +679,38 @@
     for cut in cuts:
         rs_sent(MLP, last, cut)
     out_store(last).wait()
+
+
+def hand_out(arrays):
+    n_arrays, pieces = len(arrays), arrays[0].shape[0]
+    per = [a.shape[0] // pieces for a in arrays]
+
+    def kernel(*refs):
+        srcs, dsts, bufs = (refs[i * n_arrays : (i + 1) * n_arrays] for i in range(len(refs) // n_arrays))
+        got, put = refs[n_arrays * (len(refs) // n_arrays) :]
+        order = [(i, j) for j in range(pieces) for i in range(n_arrays)]
+        rows = lambda i, j: pl.ds(j * per[i], per[i])
+        loads = [pltpu.make_async_copy(srcs[i].at[rows(i, j)], bufs[i].at[rows(i, j)], got.at[i, j]) for i, j in order]
+        stores = [pltpu.make_async_copy(bufs[i].at[rows(i, j)], dsts[i].at[rows(i, j)], put.at[i, j]) for i, j in order]
+        for cp in loads:
+            cp.start()
+        for load, store in zip(loads, stores):
+            load.wait()
+            store.start()
+        for cp in stores:
+            cp.wait()
+
+    hbm = pl.BlockSpec(memory_space=pl.ANY)
+    sems = pltpu.SemaphoreType.DMA((n_arrays, pieces))
+    return pl.pallas_call(
+        kernel,
+        in_specs=[hbm] * n_arrays,
+        out_specs=[hbm] * n_arrays,
+        out_shape=[jax.ShapeDtypeStruct(a.shape, a.dtype) for a in arrays],
+        scratch_shapes=[*[pltpu.VMEM(a.shape, a.dtype) for a in arrays], sems, sems],
+        compiler_params=pltpu.CompilerParams(vmem_limit_bytes=67_000_000),
+        name="post",
+    )(*arrays)
 
 
 def fused_layer(x, freq, b_q, b_k, b_v, k_cache, v_cache, prefix, valid, g_attn, g_mlp, w_q, w_k, w_v, w_o, w_gate, w_up, w_down, n_dev):
@@ -745,7 +777,8 @@
         compiler_params=pltpu.CompilerParams(vmem_limit_bytes=67_000_000, collective_id=0, has_side_effects=True),
         name="layer",
     )(prefix, valid, b_q, b_k, b_v, g_attn, g_mlp, freq, x.reshape(n_chunks, blk, width), k_cache, v_cache, w_q, w_k, w_v, w_o, w_gate, w_up, w_down)
-    return res[0].reshape(x.shape), res[1], res[2]
+    out, k_out, v_out = hand_out(res[:3])
+    return out.reshape(x.shape), k_out, v_out
 
 
 def solution(mesh):

time: 604 us -> 603 us (level)
  local copies, waits for them, and re-layouts: 9.13 us -> 0 us
  Pallas kernels: 594 us -> 602 us
    unnamed x7 -> x0, local copies, waits for them, and re-layouts: 9.13 us -> none
    pallas_call x0 -> x1, Pallas kernels: none -> 7.97 us  [hand_out(): pl.pallas_call(kernel, in_specs=[hbm] * n_arrays, out_specs=[hbm] * n_arr...]
where the time goes in v4:
time: 603 us; the launch traced here: 602 us
  Pallas kernels  602 us (100%)
    pallas_call x1, Pallas kernels, fused_layer(): pl.pallas_call(layer_kernel, in_specs=[smem, smem] + [vmem] * 6 + [hbm] *...  594 us

profile of v4, /device:TPU:112, one launch (start us, length us, event | category | flops | bytes accessed | tf_op | source)
XLA Modules:
  0.0 602.3 jit_solution(18131800506176298886)
XLA Ops:
  0.6 593.5 %layer.1 = (bf16[6,64,5120]{2,1,0:T(8,128)(2,1)}, bf16[12,1024,128]{2,1,0:T(8,128)(2,1)}, bf16[12,1024,128]{2,1,0:T(8,128)(2,1)}, bf16[6,8,64,5120]{3,2,1,0:T(8,...) custom-call(s32[12]{0:T(128)} %p_ref.1, s32[12]{0:T(128)} %c_ref.1, ...), custom_call_target="tpu_custom_call" | custom-call | tf_op jit(solution)/shard_map/layer/pallas_call | solution.py:771
  594.2 8.0 %post.1 = (bf16[6,64,5120]{2,1,0:T(8,128)(2,1)}, bf16[12,1024,128]{2,1,0:T(8,128)(2,1)}, bf16[12,1024,128]{2,1,0:T(8,128)(2,1)}) custom-call(bf16[6,64,5120]{2,1,0:T(8,128)(2,1)} %get-tuple-element.9.refs_0_, bf16[12,1024,128]{2,1,0:T(8,128)(2,1)} %get-tuple-element.10.refs_1_, bf16[12,1024,128]{2,1,0:T(8,128)(2,1)} %get-tuple-element.11.refs_2_), custom_call_target="tpu_custom_call" | custom-call | tf_op jit(solution)/shard_map/post/pallas_call | solution.py:705
